TPU v7x, 8 devices: a whole 2x2x1 slice. The times are simulated.
8 devices in a mesh: dp: 8 (over z, y, x, core).
Axes of the slice: x: 2, y: 2, z: 1, core: 2. Of those that a mesh axis runs over, the one named last changes fastest.
Arguments:
- token_ids: int32 [48, 512], P('dp')
- target_ids: int32 [48, 512], P('dp')
- st_wte: float32 [3, 50257, 256], P(None, None, 'dp')
- st_wpe: float32 [3, 2050, 256], P(None, None, 'dp')
- st_qkv: float32 [3, 2, 256, 3, 16, 16], P(None, None, 'dp')
- st_proj: float32 [3, 2, 16, 16, 256], P(None, None, None, None, 'dp')
- st_up: float32 [3, 2, 256, 1024], P(None, None, 'dp')
- st_down: float32 [3, 2, 1024, 256], P(None, None, 'dp')
- st_vec: float32 [3, 2, 3328], P(None, None, 'dp')
- st_lnf: float32 [3, 2, 256], P(None, None, 'dp')
Outputs:
- output 1: float32 [], replicated
- output 2: float32 [3, 50257, 256], P(None, None, 'dp')
- output 3: float32 [3, 2050, 256], P(None, None, 'dp')
- output 4: float32 [3, 2, 256, 3, 16, 16], P(None, None, 'dp')
- output 5: float32 [3, 2, 16, 16, 256], P(None, None, None, None, 'dp')
- output 6: float32 [3, 2, 256, 1024], P(None, None, 'dp')
- output 7: float32 [3, 2, 1024, 256], P(None, None, 'dp')
- output 8: float32 [3, 2, 3328], P(None, None, 'dp')
- output 9: float32 [3, 2, 256], P(None, None, 'dp')
All inputs are finite; a program needn't handle non-finite values.
Results may differ from a plain program's by a relative error of at most 0.00251365.
Values are sent between devices in bfloat16 or wider.
A program may use at most 1 GiB of HBM per device.

v0:
```python
import jax
import jax.numpy as jnp
from jax import lax
from jax.sharding import PartitionSpec as P

NORM_EPS = 1e-5
LEARN_RATE = 3e-3
BETA_ONE = 0.9
BETA_TWO = 0.95
ADAM_EPS = 1e-8
WEIGHT_DECAY = 0.1
CLIP_NORM = 1.0
ADAM_STEP = 10
DECAYS = (WEIGHT_DECAY,) * 6 + (0.0, 0.0)
LAYER_AXES = (0, 2, 0, 0, 0)


def layer_norm(residual, gain, bias):
    mean_val = jnp.mean(residual, axis=-1, keepdims=True)
    centered = residual - mean_val
    variance = jnp.mean(centered * centered, axis=-1, keepdims=True)
    return centered * lax.rsqrt(variance + NORM_EPS) * gain.astype(jnp.float32) + bias.astype(jnp.float32)


def block(residual, weights):
    qkv_w, proj_w, up_w, down_w, layer_vec = weights
    seq_len, d_model = residual.shape[1], residual.shape[2]
    num_heads, head_dim = proj_w.shape[0], proj_w.shape[1]
    offset = 4 * d_model + up_w.shape[1]
    ln_par = layer_vec[offset + d_model:].reshape(4, d_model)
    normed_in = layer_norm(residual, ln_par[0], ln_par[1]).astype(jnp.bfloat16)
    qkv_all = jnp.einsum('bsd,dthk->tbshk', normed_in, qkv_w, preferred_element_type=jnp.float32)
    qkv_all = (qkv_all + layer_vec[:3 * d_model].astype(jnp.float32).reshape(3, 1, 1, num_heads, head_dim)).astype(jnp.bfloat16)
    scores = jnp.einsum('bqhk,bshk->bhqs', qkv_all[0], qkv_all[1], preferred_element_type=jnp.float32) * head_dim ** -0.5
    rows_iota = lax.broadcasted_iota(jnp.int32, (seq_len, seq_len), 0)
    cols_iota = lax.broadcasted_iota(jnp.int32, (seq_len, seq_len), 1)
    scores = jnp.where(rows_iota >= cols_iota, scores, -1e30)
    attn_prob = jax.nn.softmax(scores, axis=-1).astype(jnp.bfloat16)
    mixed = jnp.einsum('bhqs,bshk->bqhk', attn_prob, qkv_all[2], preferred_element_type=jnp.float32).astype(jnp.bfloat16)
    residual = residual + jnp.einsum('cril,ile->cre', mixed, proj_w, preferred_element_type=jnp.float32) + layer_vec[3 * d_model:4 * d_model].astype(jnp.float32)
    normed_mid = layer_norm(residual, ln_par[2], ln_par[3]).astype(jnp.bfloat16)
    hidden = jax.nn.relu(jnp.einsum('bsd,df->bsf', normed_mid, up_w, preferred_element_type=jnp.float32) + layer_vec[4 * d_model:offset].astype(jnp.float32)).astype(jnp.bfloat16)
    return residual + jnp.einsum('bsf,fd->bsd', hidden, down_w, preferred_element_type=jnp.float32) + layer_vec[offset:offset + d_model].astype(jnp.float32)


def final_norm(residual, lnf_c):
    return layer_norm(residual, lnf_c[0], lnf_c[1]).astype(jnp.bfloat16)


def head_loss(normed, target_ids, head_w, inv_tokens):
    vocab_size, d_model = head_w.shape

    def row_step(carry, row):
        grad_acc, loss_acc = carry
        h_row, t_row = row
        logits = jnp.einsum('sd,vd->sv', h_row, head_w, preferred_element_type=jnp.float32)
        shifted = logits - jnp.max(logits, axis=-1, keepdims=True)
        exp_shift = jnp.exp(shifted)
        sum_exp = jnp.sum(exp_shift, axis=-1, keepdims=True)
        is_target = lax.broadcasted_iota(jnp.int32, logits.shape, 1) == t_row[:, None]
        picked = jnp.sum(jnp.where(is_target, shifted, 0.0), axis=-1)
        loss_acc = loss_acc + jnp.sum(jnp.log(sum_exp[:, 0]) - picked) * inv_tokens
        d_logits = ((exp_shift / sum_exp - is_target.astype(jnp.float32)) * inv_tokens).astype(jnp.bfloat16)
        grad_acc = grad_acc + jnp.einsum('sv,sd->vd', d_logits, h_row, preferred_element_type=jnp.float32)
        d_row = jnp.einsum('sv,vd->sd', d_logits, head_w, preferred_element_type=jnp.float32)
        return (grad_acc, loss_acc), d_row

    init_carry = (jnp.zeros((vocab_size, d_model), jnp.float32), jnp.zeros((), jnp.float32))
    (grad_head, loss_part), d_normed = lax.scan(row_step, init_carry, (normed, target_ids))
    return grad_head, loss_part, d_normed


def adam_update(state, grad, decay):
    moment = BETA_ONE * state[1] + (1.0 - BETA_ONE) * grad
    second = BETA_TWO * state[2] + (1.0 - BETA_TWO) * grad * grad
    m_hat = moment / (1.0 - BETA_ONE ** ADAM_STEP)
    v_hat = second / (1.0 - BETA_TWO ** ADAM_STEP)
    master = state[0] * (1.0 - LEARN_RATE * decay) - LEARN_RATE * m_hat / (jnp.sqrt(v_hat) + ADAM_EPS)
    return jnp.stack([master, moment, second])


def solution(mesh):
    n_dev = mesh.shape['dp']
    row_spec = P('dp', None)
    state_specs = (P(None, None, 'dp'), P(None, None, 'dp'), P(None, None, 'dp', None, None, None), P(None, None, None, None, 'dp'), P(None, None, 'dp', None), P(None, None, 'dp', None), P(None, None, 'dp'), P(None, None, 'dp'))

    def collect(local, axis):
        return lax.all_gather(local.astype(jnp.bfloat16), 'dp', axis=axis, tiled=True)

    def spread(full, axis):
        return lax.psum_scatter(full.astype(jnp.float32), 'dp', scatter_dimension=axis, tiled=True)

    def train_step(token_ids, target_ids, st_wte, st_wpe, st_qkv, st_proj, st_up, st_down, st_vec, st_lnf):
        num_layers = st_qkv.shape[1]
        batch_dev, seq_len = token_ids.shape
        vocab_size = st_wte.shape[1]
        pos_rows = st_wpe.shape[1]
        inv_tokens = 1.0 / (batch_dev * seq_len * n_dev)
        layer_states = (st_qkv, st_proj, st_up, st_down, st_vec)

        def layer_weights(layer):
            return tuple(collect(state[0, layer], axis) for state, axis in zip(layer_states, LAYER_AXES))

        wte_c = collect(st_wte[0], 1)
        wpe_c = collect(st_wpe[0], 1)
        residual = jnp.take(wte_c, token_ids, axis=0).astype(jnp.float32) + wpe_c[2:2 + seq_len].astype(jnp.float32)
        saved = []
        for layer in range(num_layers):
            saved.append(residual)
            residual = block(residual, layer_weights(layer))
        lnf_c = collect(st_lnf[0], 1)
        normed, norm_back = jax.vjp(final_norm, residual, lnf_c)
        head_w = collect(st_wte[0], 1)
        grad_head, loss_part, d_normed = head_loss(normed, target_ids, head_w, inv_tokens)
        d_resid, d_lnf = norm_back(d_normed.astype(jnp.bfloat16))
        layer_grads = [None] * num_layers
        for layer in reversed(range(num_layers)):
            _, block_back = jax.vjp(block, saved[layer], layer_weights(layer))
            d_resid, d_weights = block_back(d_resid)
            layer_grads[layer] = tuple(spread(grad, axis) for grad, axis in zip(d_weights, LAYER_AXES))
        d_model = d_resid.shape[-1]
        lookup_grad = jax.ops.segment_sum(d_resid.reshape(-1, d_model), token_ids.reshape(-1), num_segments=vocab_size)
        pos_grad = jnp.pad(jnp.sum(d_resid, axis=0), ((2, pos_rows - 2 - seq_len), (0, 0)))
        grads = [spread(grad_head + lookup_grad, 1), spread(pos_grad, 1)]
        for kind in range(5):
            grads.append(jnp.stack([layer_grads[layer][kind] for layer in range(num_layers)]))
        grads.append(spread(d_lnf, 1))
        local_sq = sum(jnp.sum(grad * grad) for grad in grads)
        grad_norm = jnp.sqrt(lax.psum(local_sq, 'dp'))
        clip_coef = jnp.minimum(1.0, CLIP_NORM / (grad_norm + 1e-6))
        states = (st_wte, st_wpe, st_qkv, st_proj, st_up, st_down, st_vec, st_lnf)
        new_states = tuple(adam_update(state, grad * clip_coef, decay) for state, grad, decay in zip(states, grads, DECAYS))
        loss = lax.psum(loss_part, 'dp')
        return (loss,) + new_states

    return jax.shard_map(train_step, mesh=mesh, in_specs=(row_spec, row_spec) + state_specs, out_specs=(P(),) + state_specs, check_vma=False)
```

profile of v0, /device:TPU:0, one launch (start us, length us, event | category | flops | bytes accessed | tf_op | source)
XLA Modules:
  0.0 2879.3 jit_solution(7409095365334905554)
XLA Ops:
  47.4 50.2 %all-gather.3 = bf16[1,1,256,3,16,16]{5,4,3,1,0,2:T(8,128)(2,1)S(1)} all-gather(bf16[1,1,32,3,16,16]{5,4,3,1,0,2:T(8,128)(2,1)S(1)} %get-tuple-element.168), channel_id=5, replica_groups=mesh['dp'=8] {'dp'}, dimensions={2}, use_global_device_ids=true | all-gather | bytes 442368 | tf_op jit(solution)/shard_map/all_gather | solution.py:88
  130.4 48.7 %all-gather.8 = bf16[1,1,256,3,16,16]{5,4,3,1,0,2:T(8,128)(2,1)S(1)} all-gather(bf16[1,1,32,3,16,16]{5,4,3,1,0,2:T(8,128)(2,1)S(1)} %get-tuple-element.167), channel_id=10, replica_groups=mesh['dp'=8] {'dp'}, dimensions={2}, use_global_device_ids=true | all-gather | bytes 442368 | tf_op jit(solution)/shard_map/all_gather | solution.py:88
  273.3 34.2 %copy.118 = bf16[1,50257,256]{2,1,0:T(8,128)(2,1)} copy(bf16[1,50257,256]{1,2,0:T(8,128)(2,1)} %all-gather.16.cloned.1.call-done) | data formatting | bytes 51463168 | tf_op jit(solution)/shard_map/all_gather | solution.py:88
  336.4 41.5 %fusion.291 = (f32[6,16,512]{2,1,0:T(8,128)S(1)}, f32[6,16,512,512]{2,3,1,0:T(8,128)}) fusion(pred[512,512]{0,1:T(8,128)(4,1)S(1)} %iota_compare_fusion.1, bf16[3,6,512,16,16]{2,4,3,0,1:T(8,128)(2,1)} %fusion.46), kind=kOutput, calls=%fused_computation.410 | convolution fusion | flops 905970176 | bytes 104267776 | tf_op jit(solution)/shard_map/sub | solution.py:38
  378.5 48.1 %divide_convert_fusion.1 = bf16[6,16,512,512]{2,3,1,0:T(8,128)(2,1)} fusion(f32[6,16,512,512]{2,3,1,0:T(8,128)} %get-tuple-element.196, f32[6,16,512]{2,1,0:T(8,128)S(1)} %get-tuple-element.195), kind=kLoop, calls=%fused_computation.39 | loop fusion | flops 50331648 | bytes 151191552 | tf_op jit(solution)/shard_map/convert_element_type | solution.py:38
  465.8 42.1 %fusion.294 = (f32[6,16,512]{2,1,0:T(8,128)S(1)}, f32[6,16,512,512]{2,3,1,0:T(8,128)}) fusion(pred[512,512]{0,1:T(8,128)(4,1)} %copy-done.85, bf16[3,6,512,16,16]{2,4,3,0,1:T(8,128)(2,1)} %fusion.47), kind=kOutput, calls=%fused_computation.413 | convolution fusion | flops 905970176 | bytes 104267776 | tf_op jit(solution)/shard_map/sub | solution.py:38
  508.7 48.1 %divide_convert_fusion = bf16[6,16,512,512]{2,3,1,0:T(8,128)(2,1)} fusion(f32[6,16,512,512]{2,3,1,0:T(8,128)} %get-tuple-element.202, f32[6,16,512]{2,1,0:T(8,128)S(1)} %get-tuple-element.201), kind=kLoop, calls=%fused_computation.36 | loop fusion | flops 50331648 | bytes 151191552 | tf_op jit(solution)/shard_map/convert_element_type | solution.py:38
  593.0 1224.4 %while.15 = (s32[]{:T(128)}, f32[50257,256]{1,0:T(8,128)}, f32[]{:T(128)}, bf16[6,512,256]{2,1,0:T(8,128)(2,1)}, bf16[6,512,256]{2,1,0:T(8,128)(2,1)}, /*index=5...) while((s32[]{:T(128)}, f32[50257,256]{1,0:T(8,128)}, ...), condition=%wide.region_19.20_spmd.clone, body=%wide.region_14.0_spmd.clone.sunk | while | flops 39883956224 | bytes 618661440 | solution.py:69
  593.3 43.9 %fusion.340 = (f32[512]{0:T(512)S(1)}, f32[512,50257]{0,1:T(8,128)}) fusion(bf16[50257,256]{1,0:T(8,128)(2,1)} %get-tuple-element.305, bf16[6,512,256]{2,1,0:T(8,128)(2,1)} %get-tuple-element.304, s32[]{:T(128)} %get-tuple-element.290), kind=kOutput, calls=%fused_computation.405.clone.1 | convolution fusion | flops 13200302080 | bytes 128926208 | tf_op jit(solution)/shard_map/while/body/eval_jaxpr/sd,vd->sv/dot_general | solution.py:56
  637.9 32.2 %select_reduce_fusion.2 = (f32[512]{0:T(512)S(1)}, f32[512]{0:T(512)S(1)}) fusion(f32[512,50257]{0,1:T(8,128)} %get-tuple-element.276, s32[512]{0:T(512)S(1)} %bitcast.650, f32[512]{0:T(512)S(1)} %get-tuple-element.277), kind=kLoop, calls=%fused_computation.2.clone.1 | loop fusion | flops 128656896 | bytes 102934528 | tf_op jit(solution)/shard_map/while/body/eval_jaxpr/reduce_sum | solution.py:61
  671.4 50.2 %multiply_convert_fusion.2 = bf16[512,50257]{0,1:T(8,128)(2,1)} fusion(f32[512,50257]{0,1:T(8,128)} %get-tuple-element.276, s32[512]{0:T(512)S(1)} %bitcast.651, f32[512]{0:T(512)S(1)} %get-tuple-element.278, f32[512]{0:T(512)S(1)} %get-tuple-element.277), kind=kLoop, calls=%fused_computation.3.clone.1 | loop fusion | flops 180121088 | bytes 154395648 | tf_op jit(solution)/shard_map/while/body/eval_jaxpr/convert_element_type | solution.py:63
  721.6 35.3 %convolution_add_fusion.2 = f32[50257,256]{1,0:T(8,128)} fusion(bf16[512,50257]{0,1:T(8,128)(2,1)} %multiply_convert_fusion.2, f32[50257,256]{1,0:T(8,128)} %get-tuple-element.291, pred[]{:T(512)S(6)} %compare.30, bf16[6,512,256]{2,1,0:T(8,128)(2,1)} %get-tuple-element.304, s32[]{:T(128)} %get-tuple-element.290), kind=kOutput, calls=%fused_computation.6.clone.2 | convolution fusion | flops 13200302080 | bytes 154666496 | tf_op jit(solution)/shard_map/while/body/eval_jaxpr/sv,sd->vd/dot_general | solution.py:64
  756.9 27.0 fusion.341
  783.9 43.7 %fusion.340 = (f32[512]{0:T(512)S(1)}, f32[512,50257]{0,1:T(8,128)}) fusion(bf16[50257,256]{1,0:T(8,128)(2,1)} %get-tuple-element.305, bf16[6,512,256]{2,1,0:T(8,128)(2,1)} %get-tuple-element.304, s32[]{:T(128)} %get-tuple-element.290), kind=kOutput, calls=%fused_computation.405.clone.1 | convolution fusion | flops 13200302080 | bytes 128926208 | tf_op jit(solution)/shard_map/while/body/eval_jaxpr/sd,vd->sv/dot_general | solution.py:56
  828.3 32.2 %select_reduce_fusion.2 = (f32[512]{0:T(512)S(1)}, f32[512]{0:T(512)S(1)}) fusion(f32[512,50257]{0,1:T(8,128)} %get-tuple-element.276, s32[512]{0:T(512)S(1)} %bitcast.650, f32[512]{0:T(512)S(1)} %get-tuple-element.277), kind=kLoop, calls=%fused_computation.2.clone.1 | loop fusion | flops 128656896 | bytes 102934528 | tf_op jit(solution)/shard_map/while/body/eval_jaxpr/reduce_sum | solution.py:61
  861.8 50.2 %multiply_convert_fusion.2 = bf16[512,50257]{0,1:T(8,128)(2,1)} fusion(f32[512,50257]{0,1:T(8,128)} %get-tuple-element.276, s32[512]{0:T(512)S(1)} %bitcast.651, f32[512]{0:T(512)S(1)} %get-tuple-element.278, f32[512]{0:T(512)S(1)} %get-tuple-element.277), kind=kLoop, calls=%fused_computation.3.clone.1 | loop fusion | flops 180121088 | bytes 154395648 | tf_op jit(solution)/shard_map/while/body/eval_jaxpr/convert_element_type | solution.py:63
  912.0 51.6 %convolution_add_fusion.2 = f32[50257,256]{1,0:T(8,128)} fusion(bf16[512,50257]{0,1:T(8,128)(2,1)} %multiply_convert_fusion.2, f32[50257,256]{1,0:T(8,128)} %get-tuple-element.291, pred[]{:T(512)S(6)} %compare.30, bf16[6,512,256]{2,1,0:T(8,128)(2,1)} %get-tuple-element.304, s32[]{:T(128)} %get-tuple-element.290), kind=kOutput, calls=%fused_computation.6.clone.2 | convolution fusion | flops 13200302080 | bytes 154666496 | tf_op jit(solution)/shard_map/while/body/eval_jaxpr/sv,sd->vd/dot_general | solution.py:64
  963.6 27.0 fusion.341
  990.6 43.7 %fusion.340 = (f32[512]{0:T(512)S(1)}, f32[512,50257]{0,1:T(8,128)}) fusion(bf16[50257,256]{1,0:T(8,128)(2,1)} %get-tuple-element.305, bf16[6,512,256]{2,1,0:T(8,128)(2,1)} %get-tuple-element.304, s32[]{:T(128)} %get-tuple-element.290), kind=kOutput, calls=%fused_computation.405.clone.1 | convolution fusion | flops 13200302080 | bytes 128926208 | tf_op jit(solution)/shard_map/while/body/eval_jaxpr/sd,vd->sv/dot_general | solution.py:56
  1035.1 32.2 %select_reduce_fusion.2 = (f32[512]{0:T(512)S(1)}, f32[512]{0:T(512)S(1)}) fusion(f32[512,50257]{0,1:T(8,128)} %get-tuple-element.276, s32[512]{0:T(512)S(1)} %bitcast.650, f32[512]{0:T(512)S(1)} %get-tuple-element.277), kind=kLoop, calls=%fused_computation.2.clone.1 | loop fusion | flops 128656896 | bytes 102934528 | tf_op jit(solution)/shard_map/while/body/eval_jaxpr/reduce_sum | solution.py:61
  1068.5 50.2 %multiply_convert_fusion.2 = bf16[512,50257]{0,1:T(8,128)(2,1)} fusion(f32[512,50257]{0,1:T(8,128)} %get-tuple-element.276, s32[512]{0:T(512)S(1)} %bitcast.651, f32[512]{0:T(512)S(1)} %get-tuple-element.278, f32[512]{0:T(512)S(1)} %get-tuple-element.277), kind=kLoop, calls=%fused_computation.3.clone.1 | loop fusion | flops 180121088 | bytes 154395648 | tf_op jit(solution)/shard_map/while/body/eval_jaxpr/convert_element_type | solution.py:63
  1118.8 51.6 %convolution_add_fusion.2 = f32[50257,256]{1,0:T(8,128)} fusion(bf16[512,50257]{0,1:T(8,128)(2,1)} %multiply_convert_fusion.2, f32[50257,256]{1,0:T(8,128)} %get-tuple-element.291, pred[]{:T(512)S(6)} %compare.30, bf16[6,512,256]{2,1,0:T(8,128)(2,1)} %get-tuple-element.304, s32[]{:T(128)} %get-tuple-element.290), kind=kOutput, calls=%fused_computation.6.clone.2 | convolution fusion | flops 13200302080 | bytes 154666496 | tf_op jit(solution)/shard_map/while/body/eval_jaxpr/sv,sd->vd/dot_general | solution.py:64
  1170.3 27.0 fusion.341
  1197.3 43.7 %fusion.340 = (f32[512]{0:T(512)S(1)}, f32[512,50257]{0,1:T(8,128)}) fusion(bf16[50257,256]{1,0:T(8,128)(2,1)} %get-tuple-element.305, bf16[6,512,256]{2,1,0:T(8,128)(2,1)} %get-tuple-element.304, s32[]{:T(128)} %get-tuple-element.290), kind=kOutput, calls=%fused_computation.405.clone.1 | convolution fusion | flops 13200302080 | bytes 128926208 | tf_op jit(solution)/shard_map/while/body/eval_jaxpr/sd,vd->sv/dot_general | solution.py:56
  1241.8 32.2 %select_reduce_fusion.2 = (f32[512]{0:T(512)S(1)}, f32[512]{0:T(512)S(1)}) fusion(f32[512,50257]{0,1:T(8,128)} %get-tuple-element.276, s32[512]{0:T(512)S(1)} %bitcast.650, f32[512]{0:T(512)S(1)} %get-tuple-element.277), kind=kLoop, calls=%fused_computation.2.clone.1 | loop fusion | flops 128656896 | bytes 102934528 | tf_op jit(solution)/shard_map/while/body/eval_jaxpr/reduce_sum | solution.py:61
  1275.2 50.2 %multiply_convert_fusion.2 = bf16[512,50257]{0,1:T(8,128)(2,1)} fusion(f32[512,50257]{0,1:T(8,128)} %get-tuple-element.276, s32[512]{0:T(512)S(1)} %bitcast.651, f32[512]{0:T(512)S(1)} %get-tuple-element.278, f32[512]{0:T(512)S(1)} %get-tuple-element.277), kind=kLoop, calls=%fused_computation.3.clone.1 | loop fusion | flops 180121088 | bytes 154395648 | tf_op jit(solution)/shard_map/while/body/eval_jaxpr/convert_element_type | solution.py:63
  1325.5 51.6 %convolution_add_fusion.2 = f32[50257,256]{1,0:T(8,128)} fusion(bf16[512,50257]{0,1:T(8,128)(2,1)} %multiply_convert_fusion.2, f32[50257,256]{1,0:T(8,128)} %get-tuple-element.291, pred[]{:T(512)S(6)} %compare.30, bf16[6,512,256]{2,1,0:T(8,128)(2,1)} %get-tuple-element.304, s32[]{:T(128)} %get-tuple-element.290), kind=kOutput, calls=%fused_computation.6.clone.2 | convolution fusion | flops 13200302080 | bytes 154666496 | tf_op jit(solution)/shard_map/while/body/eval_jaxpr/sv,sd->vd/dot_general | solution.py:64
  1377.0 27.0 fusion.341
  1404.0 43.7 %fusion.340 = (f32[512]{0:T(512)S(1)}, f32[512,50257]{0,1:T(8,128)}) fusion(bf16[50257,256]{1,0:T(8,128)(2,1)} %get-tuple-element.305, bf16[6,512,256]{2,1,0:T(8,128)(2,1)} %get-tuple-element.304, s32[]{:T(128)} %get-tuple-element.290), kind=kOutput, calls=%fused_computation.405.clone.1 | convolution fusion | flops 13200302080 | bytes 128926208 | tf_op jit(solution)/shard_map/while/body/eval_jaxpr/sd,vd->sv/dot_general | solution.py:56
  1448.5 32.2 %select_reduce_fusion.2 = (f32[512]{0:T(512)S(1)}, f32[512]{0:T(512)S(1)}) fusion(f32[512,50257]{0,1:T(8,128)} %get-tuple-element.276, s32[512]{0:T(512)S(1)} %bitcast.650, f32[512]{0:T(512)S(1)} %get-tuple-element.277), kind=kLoop, calls=%fused_computation.2.clone.1 | loop fusion | flops 128656896 | bytes 102934528 | tf_op jit(solution)/shard_map/while/body/eval_jaxpr/reduce_sum | solution.py:61
  1482.0 50.2 %multiply_convert_fusion.2 = bf16[512,50257]{0,1:T(8,128)(2,1)} fusion(f32[512,50257]{0,1:T(8,128)} %get-tuple-element.276, s32[512]{0:T(512)S(1)} %bitcast.651, f32[512]{0:T(512)S(1)} %get-tuple-element.278, f32[512]{0:T(512)S(1)} %get-tuple-element.277), kind=kLoop, calls=%fused_computation.3.clone.1 | loop fusion | flops 180121088 | bytes 154395648 | tf_op jit(solution)/shard_map/while/body/eval_jaxpr/convert_element_type | solution.py:63
  1532.2 51.6 %convolution_add_fusion.2 = f32[50257,256]{1,0:T(8,128)} fusion(bf16[512,50257]{0,1:T(8,128)(2,1)} %multiply_convert_fusion.2, f32[50257,256]{1,0:T(8,128)} %get-tuple-element.291, pred[]{:T(512)S(6)} %compare.30, bf16[6,512,256]{2,1,0:T(8,128)(2,1)} %get-tuple-element.304, s32[]{:T(128)} %get-tuple-element.290), kind=kOutput, calls=%fused_computation.6.clone.2 | convolution fusion | flops 13200302080 | bytes 154666496 | tf_op jit(solution)/shard_map/while/body/eval_jaxpr/sv,sd->vd/dot_general | solution.py:64
  1583.8 27.0 fusion.341
  1610.8 43.7 %fusion.340 = (f32[512]{0:T(512)S(1)}, f32[512,50257]{0,1:T(8,128)}) fusion(bf16[50257,256]{1,0:T(8,128)(2,1)} %get-tuple-element.305, bf16[6,512,256]{2,1,0:T(8,128)(2,1)} %get-tuple-element.304, s32[]{:T(128)} %get-tuple-element.290), kind=kOutput, calls=%fused_computation.405.clone.1 | convolution fusion | flops 13200302080 | bytes 128926208 | tf_op jit(solution)/shard_map/while/body/eval_jaxpr/sd,vd->sv/dot_general | solution.py:56
  1655.2 32.2 %select_reduce_fusion.2 = (f32[512]{0:T(512)S(1)}, f32[512]{0:T(512)S(1)}) fusion(f32[512,50257]{0,1:T(8,128)} %get-tuple-element.276, s32[512]{0:T(512)S(1)} %bitcast.650, f32[512]{0:T(512)S(1)} %get-tuple-element.277), kind=kLoop, calls=%fused_computation.2.clone.1 | loop fusion | flops 128656896 | bytes 102934528 | tf_op jit(solution)/shard_map/while/body/eval_jaxpr/reduce_sum | solution.py:61
  1688.7 50.2 %multiply_convert_fusion.2 = bf16[512,50257]{0,1:T(8,128)(2,1)} fusion(f32[512,50257]{0,1:T(8,128)} %get-tuple-element.276, s32[512]{0:T(512)S(1)} %bitcast.651, f32[512]{0:T(512)S(1)} %get-tuple-element.278, f32[512]{0:T(512)S(1)} %get-tuple-element.277), kind=kLoop, calls=%fused_computation.3.clone.1 | loop fusion | flops 180121088 | bytes 154395648 | tf_op jit(solution)/shard_map/while/body/eval_jaxpr/convert_element_type | solution.py:63
  1738.9 51.6 %convolution_add_fusion.2 = f32[50257,256]{1,0:T(8,128)} fusion(bf16[512,50257]{0,1:T(8,128)(2,1)} %multiply_convert_fusion.2, f32[50257,256]{1,0:T(8,128)} %get-tuple-element.291, pred[]{:T(512)S(6)} %compare.30, bf16[6,512,256]{2,1,0:T(8,128)(2,1)} %get-tuple-element.304, s32[]{:T(128)} %get-tuple-element.290), kind=kOutput, calls=%fused_computation.6.clone.2 | convolution fusion | flops 13200302080 | bytes 154666496 | tf_op jit(solution)/shard_map/while/body/eval_jaxpr/sv,sd->vd/dot_general | solution.py:64
  1790.5 27.0 fusion.341
  1862.1 50.6 %fusion.15 = (f32[6,16,512]{2,1,0:T(8,128)S(1)}, bf16[6,16,512,512]{2,3,1,0:T(8,128)(2,1)}) fusion(f32[6,16,512,512]{2,3,1,0:T(8,128)} %get-tuple-element.202, f32[6,16,512]{2,1,0:T(8,128)S(1)} %copy-done.59, bf16[3,6,512,16,16]{2,4,3,0,1:T(8,128)(2,1)} %fusion.47, bf16[6,512,16,16]{1,3,2,0:T(8,128)(2,1)S(1)} %fusion.102), kind=kOutput, calls=%fused_computation.29 | convolution fusion | flops 931086336 | bytes 154533888 | tf_op jit(solution)/shard_map/transpose(jvp(bhqs,bshk->bqhk))/dot_general | solution.py:39
  1913.4 50.0 %fusion.128 = bf16[1,6,512,16,16]{2,4,3,1,0:T(8,128)(2,1)} fusion(bf16[3,6,512,16,16]{2,4,3,0,1:T(8,128)(2,1)} %fusion.47, f32[6,16,512,512]{2,3,1,0:T(8,128)} %get-tuple-element.202, bf16[6,16,512,512]{2,3,1,0:T(8,128)(2,1)} %get-tuple-element.214, f32[6,16,512]{2,1,0:T(8,128)S(1)} %neg.29, f32[6,16,512]{2,1,0:T(8,128)S(1)} %copy-done.58, ...), kind=kOutput, calls=%fused_computation.211 | convolution fusion | flops 957087744 | bytes 154796032 | tf_op jit(solution)/shard_map/transpose(jvp(bqhk,bshk->bhqs))/dot_general | solution.py:34
  1963.4 50.2 %fusion.129 = bf16[1,6,512,16,16]{2,4,3,1,0:T(8,128)(2,1)} fusion(bf16[3,6,512,16,16]{2,4,3,0,1:T(8,128)(2,1)} %fusion.47, f32[6,16,512,512]{2,3,1,0:T(8,128)} %get-tuple-element.202, bf16[6,16,512,512]{2,3,1,0:T(8,128)(2,1)} %get-tuple-element.214, f32[6,16,512]{2,1,0:T(8,128)} %copy-done.88, f32[6,16,512]{2,1,0:T(8,128)S(1)} %copy-done.58, ...), kind=kOutput, calls=%fused_computation.212 | convolution fusion | flops 957087744 | bytes 154796032 | tf_op jit(solution)/shard_map/transpose(jvp(bqhk,bshk->bhqs))/dot_general | solution.py:34
  2041.2 50.7 %fusion.21 = (f32[6,16,512]{2,1,0:T(8,128)S(1)}, bf16[6,16,512,512]{2,3,1,0:T(8,128)(2,1)}) fusion(f32[6,16,512,512]{2,3,1,0:T(8,128)} %get-tuple-element.196, f32[6,16,512]{2,1,0:T(8,128)S(1)} %multiply_divide_fusion, bf16[3,6,512,16,16]{2,4,3,0,1:T(8,128)(2,1)} %fusion.46, bf16[6,512,16,16]{1,3,2,0:T(8,128)(2,1)S(1)} %fusion.99), kind=kOutput, calls=%fused_computation.35 | convolution fusion | flops 931086336 | bytes 154533888 | tf_op jit(solution)/shard_map/transpose(jvp(bhqs,bshk->bqhk))/dot_general | solution.py:39
  2091.9 50.2 %fusion.130 = bf16[1,6,512,16,16]{2,4,3,1,0:T(8,128)(2,1)} fusion(bf16[3,6,512,16,16]{2,4,3,0,1:T(8,128)(2,1)} %fusion.46, f32[6,16,512,512]{2,3,1,0:T(8,128)} %get-tuple-element.196, bf16[6,16,512,512]{2,3,1,0:T(8,128)(2,1)} %get-tuple-element.220, f32[6,16,512]{2,1,0:T(8,128)S(1)} %neg.32, f32[6,16,512]{2,1,0:T(8,128)S(1)} %copy-done.56, ...), kind=kOutput, calls=%fused_computation.213 | convolution fusion | flops 957087744 | bytes 154796032 | tf_op jit(solution)/shard_map/transpose(jvp(bqhk,bshk->bhqs))/dot_general | solution.py:34
  2142.1 49.9 %fusion.131 = bf16[1,6,512,16,16]{2,4,3,1,0:T(8,128)(2,1)} fusion(bf16[3,6,512,16,16]{2,4,3,0,1:T(8,128)(2,1)} %fusion.46, f32[6,16,512,512]{2,3,1,0:T(8,128)} %get-tuple-element.196, bf16[6,16,512,512]{2,3,1,0:T(8,128)(2,1)} %get-tuple-element.220, f32[6,16,512]{2,1,0:T(8,128)S(1)} %neg.32, f32[6,16,512]{2,1,0:T(8,128)S(1)} %copy-done.56, ...), kind=kOutput, calls=%fused_computation.214 | convolution fusion | flops 957087744 | bytes 154796032 | tf_op jit(solution)/shard_map/transpose(jvp(bqhk,bshk->bhqs))/dot_general | solution.py:34
  2301.1 49.7 %scatter_fusion = f32[50257,256]{1,0:T(8,128)} fusion(f32[50257,256]{1,0:T(8,128)} %get-tuple-element.49, s32[3072]{0:T(1024)S(1)} %reshape.754, f32[3072,256]{1,0:T(8,128)S(1)} %bitcast.627), kind=kCustom, calls=%fused_computation.1 | custom fusion | flops 786432 | bytes 9449472 | tf_op jit(solution)/shard_map/scatter-add | solution.py:122
  2350.8 50.9 %copy.169 = f32[50257,256]{0,1:T(8,128)} copy(f32[50257,256]{1,0:T(8,128)} %scatter_fusion) | data formatting | bytes 102926336
  2461.5 35.3 %reduce-scatter.36.cloned.1.call-done = f32[32,2050]{1,0:T(8,128)} async-done(((f32[256,2050]{1,0:T(8,128)}), f32[32,2050]{1,0:T(8,128)}) %reduce-scatter.36.cloned.1.call-update) | async-done | bytes 262416
  2498.9 275.9 %reduce-scatter.34.cloned.1.call-done = f32[32,50257]{1,0:T(8,128)} async-done(((f32[256,50257]{1,0:T(8,128)}), f32[32,50257]{1,0:T(8,128)}) %reduce-scatter.34.cloned.1.call-update) | async-done | bytes 6432912
  (591 shorter events, 613.8 us)
Async XLA Ops:
  7.2 264.7 %all-gather.18.cloned.1.call-start = ((), (), s32[]{:S(2)}) async-start(), calls=%async_computation.16 | async-start | bytes 1253376 | tf_op jit(solution)/shard_map/all_gather | solution.py:88
  8.9 264.4 %all-gather.16.cloned.1.call-start = ((), (), s32[]{:S(2)}) async-start(), calls=%async_computation.15 | async-start | bytes 28975104 | tf_op jit(solution)/shard_map/all_gather | solution.py:88
  13.8 27.8 copy-start.37
  13.8 2421.0 %reduce-scatter.46.cloned.1.call-start = ((), (), s32[]{:S(2)}) async-start(), calls=%async_computation.23 | async-start | bytes 147456
  100.7 26.8 copy-start.43
  100.7 27.6 copy-start.42
  100.7 28.4 copy-start.144
  182.3 87.1 %copy-start.118 = (bf16[1,1,3328]{2,1,0:T(2,128)(2,1)S(1)}, bf16[1,1,3328]{2,1,0:T(2,128)(2,1)}, u32[]{:S(2)}) copy-start(bf16[1,1,3328]{2,1,0:T(2,128)(2,1)} %copy-done.117) | copy-start | bytes 19972
  182.3 87.7 %copy-start.120 = (bf16[1,1,3328]{2,1,0:T(2,128)(2,1)S(1)}, bf16[1,1,3328]{2,1,0:T(2,128)(2,1)}, u32[]{:S(2)}) copy-start(bf16[1,1,3328]{2,1,0:T(2,128)(2,1)} %copy-done.119) | copy-start | bytes 19972
  182.3 89.6 %copy-start.123 = (s32[3072]{0:T(1024)S(1)}, s32[3072]{0:T(1024)}, u32[]{:S(2)}) copy-start(s32[3072]{0:T(1024)} %reshape.746) | copy-start | bytes 36868
  268.8 67.6 %copy-start.85 = (pred[512,512]{0,1:T(8,128)(4,1)}, pred[512,512]{0,1:T(8,128)(4,1)S(1)}, u32[]{:S(2)}) copy-start(pred[512,512]{0,1:T(8,128)(4,1)S(1)} %iota_compare_fusion.1) | copy-start | bytes 786436
  270.0 61.8 %copy-start.133 = (f32[1,1,256]{2,1,0:T(1,128)}, f32[1,1,256]{2,1,0:T(1,128)S(1)}, u32[]{:S(2)}) copy-start(f32[1,1,256]{2,1,0:T(1,128)S(1)} %get-tuple-element.189) | copy-start | bytes 3076
  270.0 61.8 %copy-start.160 = (f32[1,1,256]{2,1,0:T(1,128)}, f32[1,1,256]{2,1,0:T(1,128)S(1)}, u32[]{:S(2)}) copy-start(f32[1,1,256]{2,1,0:T(1,128)S(1)} %get-tuple-element.188) | copy-start | bytes 3076
  271.8 175.4 %copy-start.112 = (pred[6,512]{1,0:T(8,128)(4,1)}, pred[6,512]{1,0:T(8,128)(4,1)S(1)}, u32[]{:S(2)}) copy-start(pred[6,512]{1,0:T(8,128)(4,1)S(1)} %compare_and_fusion) | copy-start | bytes 9220
  273.2 174.0 %copy-start.29 = (f32[512,256]{1,0:T(8,128)}, f32[512,256]{1,0:T(8,128)S(1)}, u32[]{:S(2)}) copy-start(f32[512,256]{1,0:T(8,128)S(1)} %copy.119) | copy-start | bytes 1572868
  328.9 118.3 %copy-start.17 = (bf16[3072,256]{1,0:T(8,128)(2,1)}, bf16[3072,256]{1,0:T(8,128)(2,1)S(1)}, u32[]{:S(2)}) copy-start(bf16[3072,256]{1,0:T(8,128)(2,1)S(1)} %gather_fusion) | copy-start | bytes 4718596
  426.6 20.6 copy-start.51
  426.6 20.6 copy-start.163
  460.0 117.4 %copy-start.8 = (f32[6,512,256]{2,1,0:T(8,128)}, f32[6,512,256]{2,1,0:T(8,128)S(1)}, u32[]{:S(2)}) copy-start(f32[6,512,256]{2,1,0:T(8,128)S(1)} %get-tuple-element.200) | copy-start | bytes 9437188
  556.8 20.7 copy-start.53
  556.8 20.7 copy-start.162
  593.0 1224.5 %copy-start.1 = (f32[6,512,256]{2,1,0:T(8,128)S(1)}, f32[6,512,256]{2,1,0:T(8,128)}, u32[]{:S(2)}) copy-start(f32[6,512,256]{2,1,0:T(8,128)} %copy-done) | copy-start | bytes 9437188
  593.0 1224.5 %copy-start.69 = (f32[6,512]{1,0:T(8,128)S(1)}, f32[6,512]{1,0:T(8,128)}, u32[]{:S(2)}) copy-start(f32[6,512]{1,0:T(8,128)} %copy-done.68) | copy-start | bytes 36868
  593.0 1224.5 %copy-start.132 = (f32[1,256]{1,0:T(1,128)S(1)}, f32[1,256]{1,0:T(1,128)}, u32[]{:S(2)}) copy-start(f32[1,256]{1,0:T(1,128)} %get-tuple-element.193) | copy-start | bytes 3076
  1841.0 21.1 copy-start.59
  1862.1 51.3 %copy-start.58 = (f32[6,16,512]{2,1,0:T(8,128)S(1)}, f32[6,16,512]{2,1,0:T(8,128)}, u32[]{:S(2)}) copy-start(f32[6,16,512]{2,1,0:T(8,128)} %copy-done.57) | copy-start | bytes 589828
  1862.1 51.3 %copy-start.86 = (pred[512,512]{0,1:T(8,128)(4,1)S(1)}, pred[512,512]{0,1:T(8,128)(4,1)}, u32[]{:S(2)}) copy-start(pred[512,512]{0,1:T(8,128)(4,1)} %copy-done.85) | copy-start | bytes 786436
  1963.4 50.2 %copy-start.56 = (f32[6,16,512]{2,1,0:T(8,128)S(1)}, f32[6,16,512]{2,1,0:T(8,128)}, u32[]{:S(2)}) copy-start(f32[6,16,512]{2,1,0:T(8,128)} %copy-done.55) | copy-start | bytes 589828
  1963.4 50.3 %copy-start.9 = (f32[6,512,256]{2,1,0:T(8,128)S(1)}, f32[6,512,256]{2,1,0:T(8,128)}, u32[]{:S(2)}) copy-start(f32[6,512,256]{2,1,0:T(8,128)} %copy-done.8) | copy-start | bytes 9437188
  1963.4 50.3 %copy-start.81 = (f32[6,512]{1,0:T(8,128)S(1)}, f32[6,512]{1,0:T(8,128)}, u32[]{:S(2)}) copy-start(f32[6,512]{1,0:T(8,128)} %copy-done.80) | copy-start | bytes 36868
  2041.2 50.8 %copy-start.20 = (bf16[6,512,16,16]{1,3,2,0:T(8,128)(2,1)}, bf16[6,512,16,16]{1,3,2,0:T(8,128)(2,1)S(1)}, u32[]{:S(2)}) copy-start(bf16[6,512,16,16]{1,3,2,0:T(8,128)(2,1)S(1)} %fusion.99) | copy-start | bytes 4718596
  2041.2 50.8 %copy-start.87 = (pred[512,512]{0,1:T(8,128)(4,1)S(1)}, pred[512,512]{0,1:T(8,128)(4,1)}, u32[]{:S(2)}) copy-start(pred[512,512]{0,1:T(8,128)(4,1)} %copy-done.85) | copy-start | bytes 786436
  2142.1 49.9 %copy-start.167 = (bf16[256]{0:T(256)(128)(2,1)S(1)}, bf16[256]{0:T(256)(128)(2,1)}, u32[]{:S(2)}) copy-start(bf16[256]{0:T(256)(128)(2,1)} %get-tuple-element.110) | copy-start | bytes 1540
  2142.1 52.6 %copy-start.12 = (f32[6,512,256]{2,1,0:T(8,128)S(1)}, f32[6,512,256]{2,1,0:T(8,128)}, u32[]{:S(2)}) copy-start(f32[6,512,256]{2,1,0:T(8,128)} %copy-done.11) | copy-start | bytes 9437188
  2194.7 241.6 %reduce-scatter.42.cloned.1.call-start = ((), (), s32[]{:S(2)}) async-start(), calls=%async_computation.21 | async-start | bytes 294912
  2199.6 21.7 copy-start.16
  2199.6 237.7 %reduce-scatter.44.cloned.1.call-start = ((), (), s32[]{:S(2)}) async-start(), calls=%async_computation.22 | async-start | bytes 294912
  2228.9 210.2 %reduce-scatter.38.cloned.1.call-start = ((), (), s32[]{:S(2)}) async-start(), calls=%async_computation.19 | async-start | bytes 884736
  2238.6 201.6 %reduce-scatter.40.cloned.1.call-start = ((), (), s32[]{:S(2)}) async-start(), calls=%async_computation.20 | async-start | bytes 884736
  2246.8 195.2 %reduce-scatter.30.cloned.1.call-start = ((), (), s32[]{:S(2)}) async-start(), calls=%async_computation.13 | async-start | bytes 1179648 | tf_op jit(solution)/shard_map/reduce_scatter | solution.py:91
  2254.4 187.7 %reduce-scatter.32.cloned.1.call-start = ((), (), s32[]{:S(2)}) async-start(), calls=%async_computation.14 | async-start | bytes 1179648 | tf_op jit(solution)/shard_map/reduce_scatter | solution.py:91
  2263.5 180.2 %reduce-scatter.26.cloned.1.call-start = ((), (), s32[]{:S(2)}) async-start(), calls=%async_computation.11 | async-start | bytes 1179648 | tf_op jit(solution)/shard_map/reduce_scatter | solution.py:91
  2270.7 189.1 %reduce-scatter.28.cloned.1.call-start = ((), (), s32[]{:S(2)}) async-start(), calls=%async_computation.12 | async-start | bytes 1179648 | tf_op jit(solution)/shard_map/reduce_scatter | solution.py:91
  2283.7 213.1 %reduce-scatter.36.cloned.1.call-start = ((), (), s32[]{:S(2)}) async-start(), calls=%async_computation.18 | async-start | bytes 2506752
  2301.0 473.8 %reduce-scatter.34.cloned.1.call-start = ((), (), s32[]{:S(2)}) async-start(), calls=%async_computation.17 | async-start | bytes 57950208
  2789.5 42.7 %copy-start.122 = (f32[3,2,416]{2,1,0:T(2,128)S(1)}, f32[3,2,416]{2,1,0:T(2,128)}, u32[]{:S(2)}) copy-start(f32[3,2,416]{2,1,0:T(2,128)} %param.20) | copy-start | bytes 29956
  2789.5 43.4 %copy-start.67 = (f32[128,256]{1,0:T(8,128)S(1)}, f32[128,256]{1,0:T(8,128)}, u32[]{:S(2)}) copy-start(f32[128,256]{1,0:T(8,128)} %reduce-scatter.30.cloned.1.call-done) | copy-start | bytes 393220
  2802.4 33.5 %copy-start.38 = (f32[3,2,32,3,16,16]{2,5,4,3,1,0:T(8,128)S(1)}, f32[3,2,32,3,16,16]{2,5,4,3,1,0:T(8,128)}, u32[]{:S(2)}) copy-start(f32[3,2,32,3,16,16]{2,5,4,3,1,0:T(8,128)} %param.16) | copy-start | bytes 1769476
  (137 other events, 511.6 us)
Sparse Core Ops, SparseCore 0:
  10.4 20.9 all-gather.17
  33.7 174.6 all-gather.15
  2194.8 25.3 reduce-scatter.45
  2223.0 25.4 reduce-scatter.41
  2251.3 25.3 reduce-scatter.43
  2280.2 26.4 reduce-scatter.37
  2310.4 26.5 reduce-scatter.39
  2340.0 27.5 reduce-scatter.29
  2370.7 27.5 reduce-scatter.31
  2401.3 27.7 reduce-scatter.25
  2432.2 27.6 reduce-scatter.27
  2463.5 33.2 reduce-scatter.35
  2500.4 274.4 reduce-scatter.33
where the time goes:
time: 2890 us; the launch traced here: 2880 us
  matrix products  1280 us (44%)
  other arithmetic  772 us (27%)
  waiting for transfers between devices  328 us (11%)
  blocking collectives  274 us (9%)
  local copies, waits for them, and re-layouts  197 us (7%)
    unnamed x20, waiting for transfers between devices  311 us
    convert_element_type x6, other arithmetic, row_step(): ((exp_shift / sum_exp - is_target.astype(jnp.float32)) * inv_tokens).asty...  301 us
    dot_general x6, matrix products, row_step(): jnp.einsum('sv,sd->vd', d_logits, h_row, preferred_element_type=jnp.float32)  293 us
    dot_general x6, matrix products, row_step(): jnp.einsum('sd,vd->sv', h_row, head_w, preferred_element_type=jnp.float32)  262 us
    all_gather x9, blocking collectives, collect(): lax.all_gather(local.astype(jnp.bfloat16), 'dp', axis=axis, tiled=True)  203 us
    dot_general x4, matrix products, block(): jnp.einsum('bqhk,bshk->bhqs', qkv_all[0], qkv_all[1], preferred_element_t...  200 us
    reduce_sum x6, other arithmetic, row_step(): picked = jnp.sum(jnp.where(is_target, shifted, 0.0), axis=-1)  193 us
    dot_general x6, matrix products, block(): jnp.einsum('bhqs,bshk->bqhk', attn_prob, qkv_all[2], preferred_element_ty...  185 us
  transfers between devices with their start and end apart: 13, of which 3 were waited for; matrix products, arithmetic and copies ran while one was open for 9% of the time, Pallas kernels for 0%

commit v1 on v0

v1 whole, which is shorter than its diff:
```python
import functools

import jax
import jax.numpy as jnp
from jax import lax
from jax.experimental import pallas as pl
from jax.experimental.pallas import tpu as pltpu
from jax.sharding import PartitionSpec as P

NORM_EPS = 1e-5
LEARN_RATE = 3e-3
BETA_ONE = 0.9
BETA_TWO = 0.95
ADAM_EPS = 1e-8
WEIGHT_DECAY = 0.1
CLIP_NORM = 1.0
ADAM_STEP = 10
DECAYS = (WEIGHT_DECAY,) * 6 + (0.0, 0.0)
VOCAB_TILE = 1536
TOKEN_TILE = 3072
LSE_CHUNK = 128
GRAD_CHUNK = 256
N_ACC = 8
HEADS_STEP = 2
LOWEST = -3.0e38
BIG_VMEM = 60 * 1024 * 1024
F32 = jnp.float32
BF16 = jnp.bfloat16


def layer_norm(residual, gain, bias):
    mean_val = jnp.mean(residual, axis=-1, keepdims=True)
    centered = residual - mean_val
    variance = jnp.mean(centered * centered, axis=-1, keepdims=True)
    return centered * lax.rsqrt(variance + NORM_EPS) * gain.astype(F32) + bias.astype(F32)


def dot(a, b):
    return jnp.dot(a, b, preferred_element_type=F32)


def attn_fwd_kernel(qkv_ref, o_ref, lse_ref, qt_ref, vt_ref, ot_ref, *, seq, dm, hd):
    qt_ref[...] = (qkv_ref[0, :, :dm] * jnp.asarray(hd ** -0.5, BF16)).T
    vt_ref[...] = qkv_ref[0, :, 2 * dm:].T
    half = seq // 2
    per = 128 // hd
    lo, hi = slice(0, half), slice(half, seq)
    row_head = lax.broadcasted_iota(jnp.int32, (128, seq), 0) // hd
    keep = lax.broadcasted_iota(jnp.int32, (half, half), 0) <= lax.broadcasted_iota(jnp.int32, (half, half), 1)
    for slab in range(dm // 128):
        base = slab * 128

        @pl.loop(0, per // HEADS_STEP)
        def _(i):
            todo = []
            for j in range(HEADS_STEP):
                hh = i * HEADS_STEP + j
                qm = jnp.where(row_head == hh, qt_ref[base:base + 128, :], jnp.zeros((), BF16))
                k_lo = qkv_ref[0, lo, dm + base:dm + base + 128]
                k_hi = qkv_ref[0, hi, dm + base:dm + base + 128]
                both = dot(k_lo, qm)
                diag = dot(k_hi, qm[:, hi])
                todo.append((hh, both[:, lo], both[:, hi], diag))
            for hh, s00, s01, s11 in todo:
                rows = pl.ds(pl.multiple_of(base + hh * hd, hd), hd)
                stat = pl.ds(slab * per + hh, 1)
                s00 = jnp.where(keep, s00, -1e30)
                s11 = jnp.where(keep, s11, -1e30)
                m0 = jnp.max(s00, axis=0, keepdims=True)
                e00 = jnp.exp(s00 - m0)
                l0 = jnp.sum(e00, axis=0, keepdims=True)
                m1 = jnp.maximum(jnp.max(s01, axis=0, keepdims=True), jnp.max(s11, axis=0, keepdims=True))
                e01 = jnp.exp(s01 - m1)
                e11 = jnp.exp(s11 - m1)
                l1 = jnp.sum(e01, axis=0, keepdims=True) + jnp.sum(e11, axis=0, keepdims=True)
                inv0, inv1 = 1.0 / l0, 1.0 / l1
                p00 = (e00 * inv0).astype(BF16)
                p01 = (e01 * inv1).astype(BF16)
                p11 = (e11 * inv1).astype(BF16)
                ot_ref[rows, lo] = dot(vt_ref[rows, lo], p00)
                ot_ref[rows, hi] = dot(vt_ref[rows, lo], p01) + dot(vt_ref[rows, hi], p11)
                lse_ref[0, stat, lo] = m0 + jnp.log(l0)
                lse_ref[0, stat, hi] = m1 + jnp.log(l1)

    o_ref[0] = ot_ref[...].T.astype(BF16)


def attn_bwd_kernel(qkv_ref, do_ref, lse_ref, dqkv_ref, qt_ref, kt_ref, dot_ref, dqt_ref, dk_ref, dv_ref, *, seq, dm, hd):
    scale = hd ** -0.5
    qt_ref[...] = (qkv_ref[0, :, :dm] * jnp.asarray(scale, BF16)).T
    kt_ref[...] = qkv_ref[0, :, dm:2 * dm].T
    dot_ref[...] = do_ref[0].T
    dk_ref[...] = jnp.zeros_like(dk_ref)
    dv_ref[...] = jnp.zeros_like(dv_ref)
    half = seq // 2
    per = 128 // hd
    lo, hi = slice(0, half), slice(half, seq)
    zero = jnp.zeros((), BF16)
    row_head = lax.broadcasted_iota(jnp.int32, (128, seq), 0) // hd
    lane_head = lax.broadcasted_iota(jnp.int32, (seq, 128), 1) // hd
    keep = lax.broadcasted_iota(jnp.int32, (half, half), 0) <= lax.broadcasted_iota(jnp.int32, (half, half), 1)
    for slab in range(dm // 128):
        base = slab * 128
        lanes = slice(base, base + 128)
        k_at = slice(dm + base, dm + base + 128)
        v_at = slice(2 * dm + base, 2 * dm + base + 128)

        @pl.loop(0, per // HEADS_STEP)
        def _(i):
            todo = []
            for j in range(HEADS_STEP):
                hh = i * HEADS_STEP + j
                qm = jnp.where(row_head == hh, qt_ref[lanes, :], zero)
                dom = jnp.where(row_head == hh, dot_ref[lanes, :], zero)
                s_lo = dot(qkv_ref[0, lo, k_at], qm)
                s_hi = dot(qkv_ref[0, hi, k_at], qm[:, hi])
                dp_lo = dot(qkv_ref[0, lo, v_at], dom)
                dp_hi = dot(qkv_ref[0, hi, v_at], dom[:, hi])
                todo.append((hh, s_lo, s_hi, dp_lo, dp_hi))
            for hh, s_lo, s_hi, dp_lo, dp_hi in todo:
                rows = pl.ds(pl.multiple_of(base + hh * hd, hd), hd)
                lse = lse_ref[0, pl.ds(slab * per + hh, 1), :]
                q_lane = jnp.where(lane_head == hh, qkv_ref[0, :, lanes], zero)
                do_lane = jnp.where(lane_head == hh, do_ref[0, :, lanes], zero)
                p00 = jnp.exp(jnp.where(keep, s_lo[:, lo], -1e30) - lse[:, lo])
                p01 = jnp.exp(s_lo[:, hi] - lse[:, hi])
                p11 = jnp.exp(jnp.where(keep, s_hi, -1e30) - lse[:, hi])
                w00, w01, w11 = p00 * dp_lo[:, lo], p01 * dp_lo[:, hi], p11 * dp_hi
                delta0 = jnp.sum(w00, axis=0, keepdims=True)
                delta1 = jnp.sum(w01, axis=0, keepdims=True) + jnp.sum(w11, axis=0, keepdims=True)
                ds_lo = jnp.concatenate([(w00 - p00 * delta0).astype(BF16), (w01 - p01 * delta1).astype(BF16)], axis=1)
                ds_hi = (w11 - p11 * delta1).astype(BF16)
                p_lo = jnp.concatenate([p00.astype(BF16), p01.astype(BF16)], axis=1)
                dv_ref[lo, lanes] += dot(p_lo, do_lane)
                dv_ref[hi, lanes] += dot(p11.astype(BF16), do_lane[hi, :])
                dk_ref[lo, lanes] += dot(ds_lo, q_lane)
                dk_ref[hi, lanes] += dot(ds_hi, q_lane[hi, :])
                dq = dot(kt_ref[rows, lo], ds_lo)
                dqt_ref[rows, lo] = dq[:, lo]
                dqt_ref[rows, hi] = dq[:, hi] + dot(kt_ref[rows, hi], ds_hi)

    dqkv_ref[0, :, :dm] = (dqt_ref[...] * scale).T.astype(BF16)
    dqkv_ref[0, :, dm:2 * dm] = (dk_ref[...] * scale).astype(BF16)
    dqkv_ref[0, :, 2 * dm:] = dv_ref[...].astype(BF16)


def attn_fwd_call(qkv, n_heads):
    batch, seq, three = qkv.shape
    dm = three // 3
    flops = 4 * batch * n_heads * seq * seq * 128
    return pl.pallas_call(
        functools.partial(attn_fwd_kernel, seq=seq, dm=dm, hd=dm // n_heads),
        grid=(batch,),
        in_specs=[pl.BlockSpec((1, seq, three), lambda b: (b, 0, 0))],
        out_specs=[pl.BlockSpec((1, seq, dm), lambda b: (b, 0, 0)), pl.BlockSpec((1, n_heads, seq), lambda b: (b, 0, 0))],
        out_shape=[jax.ShapeDtypeStruct((batch, seq, dm), BF16), jax.ShapeDtypeStruct((batch, n_heads, seq), F32)],
        scratch_shapes=[pltpu.VMEM((dm, seq), BF16), pltpu.VMEM((dm, seq), BF16), pltpu.VMEM((dm, seq), F32)],
        cost_estimate=pl.CostEstimate(flops=flops, bytes_accessed=qkv.size * 3, transcendentals=0),
        name="attn_fwd",
    )(qkv)


def attn_bwd_call(qkv, d_o, lse, n_heads):
    batch, seq, three = qkv.shape
    dm = three // 3
    flops = 10 * batch * n_heads * seq * seq * 128
    return pl.pallas_call(
        functools.partial(attn_bwd_kernel, seq=seq, dm=dm, hd=dm // n_heads),
        grid=(batch,),
        in_specs=[pl.BlockSpec((1, seq, three), lambda b: (b, 0, 0)), pl.BlockSpec((1, seq, dm), lambda b: (b, 0, 0)), pl.BlockSpec((1, n_heads, seq), lambda b: (b, 0, 0))],
        out_specs=pl.BlockSpec((1, seq, three), lambda b: (b, 0, 0)),
        out_shape=jax.ShapeDtypeStruct((batch, seq, three), BF16),
        scratch_shapes=[pltpu.VMEM((dm, seq), BF16), pltpu.VMEM((dm, seq), BF16), pltpu.VMEM((dm, seq), BF16), pltpu.VMEM((dm, seq), F32), pltpu.VMEM((seq, dm), F32), pltpu.VMEM((seq, dm), F32)],
        cost_estimate=pl.CostEstimate(flops=flops, bytes_accessed=qkv.size * 6, transcendentals=0),
        name="attn_bwd",
    )(qkv, d_o, lse)


@functools.partial(jax.custom_vjp, nondiff_argnums=(1,))
def attention(qkv, n_heads):
    return attn_fwd_call(qkv, n_heads)[0]


def attention_fwd(qkv, n_heads):
    out, lse = attn_fwd_call(qkv, n_heads)
    return out, (qkv, lse)


def attention_bwd(n_heads, saved, d_o):
    qkv, lse = saved
    return (attn_bwd_call(qkv, d_o.astype(BF16), lse, n_heads),)


attention.defvjp(attention_fwd, attention_bwd)


def block(residual, weights, n_heads):
    qkv_w, proj_w, up_w, down_w, layer_vec = weights
    d_model = residual.shape[-1]
    offset = 4 * d_model + up_w.shape[1]
    ln_par = layer_vec[offset + d_model:].reshape(4, d_model)
    normed_in = layer_norm(residual, ln_par[0], ln_par[1]).astype(BF16)
    qkv = (jnp.einsum('bsd,dn->bsn', normed_in, qkv_w, preferred_element_type=F32) + layer_vec[:3 * d_model].astype(F32)).astype(BF16)
    mixed = attention(qkv, n_heads)
    residual = residual + jnp.einsum('bsd,de->bse', mixed, proj_w, preferred_element_type=F32) + layer_vec[3 * d_model:4 * d_model].astype(F32)
    normed_mid = layer_norm(residual, ln_par[2], ln_par[3]).astype(BF16)
    hidden = jax.nn.relu(jnp.einsum('bsd,df->bsf', normed_mid, up_w, preferred_element_type=F32) + layer_vec[4 * d_model:offset].astype(F32)).astype(BF16)
    return residual + jnp.einsum('bsf,fd->bsd', hidden, down_w, preferred_element_type=F32) + layer_vec[offset:offset + d_model].astype(F32)


def final_norm(residual, lnf_c):
    return layer_norm(residual, lnf_c[0], lnf_c[1]).astype(BF16)


def lse_kernel(h_ref, w_ref, lse_ref, m_ref, s_ref, *, vocab, tile):
    v = pl.program_id(0)
    t = pl.program_id(1)
    n_rows = h_ref.shape[0]
    n_chunk = n_rows // LSE_CHUNK
    last = pl.num_programs(0) - 1

    @pl.when(v == 0)
    def _():
        m_ref[t] = jnp.full(m_ref.shape[1:], -jnp.inf, F32)
        s_ref[t] = jnp.zeros(s_ref.shape[1:], F32)

    def work(masked):
        def product(c):
            return dot(h_ref[c * LSE_CHUNK:(c + 1) * LSE_CHUNK, :], w_ref[...])

        ahead = product(0)
        for c in range(n_chunk):
            logits = ahead
            if c + 1 < n_chunk:
                ahead = product(c + 1)
            part = slice(c * LSE_CHUNK, (c + 1) * LSE_CHUNK)
            if masked:
                ids = lax.broadcasted_iota(jnp.int32, logits.shape, 1) + v * tile
                logits = jnp.where(ids < vocab, logits, -jnp.inf)
            cols = [logits[:, k * 128:(k + 1) * 128] for k in range(tile // 128)]
            m_old = m_ref[t, part, :]
            m_new = m_old
            for x in cols:
                m_new = jnp.maximum(m_new, x)
            s_new = s_ref[t, part, :] * jnp.exp(m_old - jnp.maximum(m_new, LOWEST))
            m_safe = jnp.maximum(m_new, LOWEST)
            for x in cols:
                s_new = s_new + jnp.exp(x - m_safe)
            m_ref[t, part, :] = m_new
            s_ref[t, part, :] = s_new

    @pl.when(v < last)
    def _():
        work(False)

    @pl.when(v == last)
    def _():
        work(True)
        rows = pl.ds(pl.multiple_of(t * n_rows, n_rows), n_rows)
        m_lane = m_ref[t]
        m = jnp.max(m_lane, axis=1, keepdims=True)
        total = jnp.sum(s_ref[t] * jnp.exp(m_lane - m), axis=1, keepdims=True)
        lse_ref[rows, :] = m + jnp.log(total)


def grad_kernel(h_ref, ht_ref, w_ref, lse_ref, tgt_ref, dh_ref, dw_ref, pick_ref, wt_ref, d_ref, *, tile, inv_tokens):
    v = pl.program_id(0)
    t = pl.program_id(1)
    n_rows = h_ref.shape[0]
    n_chunk = n_rows // GRAD_CHUNK

    @pl.when(t == 0)
    def _():
        wt_ref[...] = w_ref[...].T

    @pl.when(v == 0)
    def _():
        dh_ref[t] = jnp.zeros(dh_ref.shape[1:], F32)
        pick_ref[t] = jnp.zeros(pick_ref.shape[1:], F32)

    def product(c):
        return dot(h_ref[c * GRAD_CHUNK:(c + 1) * GRAD_CHUNK, :], w_ref[...])

    ahead = product(0)
    lane = lax.broadcasted_iota(jnp.int32, (GRAD_CHUNK, 128), 1)
    for c in range(n_chunk):
        logits = ahead
        if c + 1 < n_chunk:
            ahead = product(c + 1)
        part = slice(c * GRAD_CHUNK, (c + 1) * GRAD_CHUNK)
        lse = jnp.broadcast_to(lse_ref[part, :], (GRAD_CHUNK, 128))
        place = jnp.broadcast_to(tgt_ref[part, :] - v * tile, (GRAD_CHUNK, 128)) - lane
        pick = pick_ref[t, part, :]
        for k in range(tile // 128):
            shifted = jnp.minimum(logits[:, k * 128:(k + 1) * 128] - lse, 0.0)
            hit = place == k * 128
            pick = jnp.where(hit, shifted, pick)
            prob = jnp.exp(shifted)
            d_ref[part, k * 128:(k + 1) * 128] = jnp.where(hit, prob - 1.0, prob).astype(BF16)
        pick_ref[t, part, :] = pick
        dh_ref[t, part, :] += dot(d_ref[part, :], wt_ref[...])
    term = dot(ht_ref[...], d_ref[...]) * inv_tokens

    @pl.when(t == 0)
    def _():
        dw_ref[...] = term

    @pl.when(t > 0)
    def _():
        dw_ref[...] += term


def head_loss(normed, target_ids, head_t, vocab, inv_tokens):
    n_tok, dm = normed.shape
    padded = head_t.shape[1]
    n_v, n_t = padded // VOCAB_TILE, n_tok // TOKEN_TILE
    flops = 2 * n_tok * padded * dm
    h_spec = pl.BlockSpec((TOKEN_TILE, dm), lambda v, t: (t, 0))
    w_spec = pl.BlockSpec((dm, VOCAB_TILE), lambda v, t: (0, v))
    col_spec = pl.BlockSpec((TOKEN_TILE, 1), lambda v, t: (t, 0))
    full_col = pl.BlockSpec((n_tok, 1), lambda v, t: (0, 0))
    lse = pl.pallas_call(
        functools.partial(lse_kernel, vocab=vocab, tile=VOCAB_TILE),
        grid=(n_v, n_t),
        in_specs=[h_spec, w_spec],
        out_specs=full_col,
        out_shape=jax.ShapeDtypeStruct((n_tok, 1), F32),
        scratch_shapes=[pltpu.VMEM((n_t, TOKEN_TILE, 128), F32), pltpu.VMEM((n_t, TOKEN_TILE, 128), F32)],
        compiler_params=pltpu.CompilerParams(vmem_limit_bytes=BIG_VMEM),
        cost_estimate=pl.CostEstimate(flops=flops, bytes_accessed=head_t.size * 2, transcendentals=0),
        name="head_lse",
    )(normed, head_t)
    d_h, d_w, picked = pl.pallas_call(
        functools.partial(grad_kernel, tile=VOCAB_TILE, inv_tokens=inv_tokens),
        grid=(n_v, n_t),
        in_specs=[h_spec, pl.BlockSpec((dm, TOKEN_TILE), lambda v, t: (0, t)), w_spec, col_spec, col_spec],
        out_specs=[pl.BlockSpec((n_t, TOKEN_TILE, dm), lambda v, t: (0, 0, 0)), w_spec, pl.BlockSpec((n_t, TOKEN_TILE, 128), lambda v, t: (0, 0, 0))],
        out_shape=[jax.ShapeDtypeStruct((n_t, TOKEN_TILE, dm), F32), jax.ShapeDtypeStruct((dm, padded), F32), jax.ShapeDtypeStruct((n_t, TOKEN_TILE, 128), F32)],
        scratch_shapes=[pltpu.VMEM((VOCAB_TILE, dm), BF16), pltpu.VMEM((TOKEN_TILE, VOCAB_TILE), BF16)],
        compiler_params=pltpu.CompilerParams(vmem_limit_bytes=BIG_VMEM),
        cost_estimate=pl.CostEstimate(flops=3 * flops, bytes_accessed=head_t.size * 6, transcendentals=0),
        name="head_grad",
    )(normed, normed.T, head_t, lse, target_ids.reshape(n_tok, 1))
    return d_w, -jnp.sum(picked) * inv_tokens, d_h.reshape(n_tok, dm) * inv_tokens


def gather_kernel(code_ref, table_ref, out_ref, wide_ref, *, width):
    groups = 128 // width
    lane_group = lax.broadcasted_iota(jnp.int32, (1, 128), 1) // width

    @pl.loop(0, out_ref.shape[0] // 16)
    def _(i):
        for j in range(16):
            pos = i * 16 + j
            code = code_ref[0, 0, pos]
            row = table_ref[pl.ds(code >> 2, 1), :]
            wide_ref[pl.ds(pos, 1), :] = jnp.where(lane_group == (code & 3), row, 0.0)

    from_lane = lax.broadcasted_iota(jnp.int32, (128, width), 0) % width
    fold = (from_lane == lax.broadcasted_iota(jnp.int32, (128, width), 1)).astype(F32).astype(BF16)
    out_ref[...] = dot(wide_ref[...].astype(BF16), fold).astype(BF16)


def scatter_kernel(code_ref, dx_ref, out_ref, wide_ref, *accs, width):
    step = pl.program_id(0)
    groups = 128 // width
    lane_group = lax.broadcasted_iota(jnp.int32, (1, 128), 1) // width

    @pl.when(step == 0)
    def _():
        for acc in accs:
            acc[...] = jnp.zeros_like(acc)

    wide_ref[...] = jnp.concatenate([dx_ref[...]] * groups, axis=1)

    @pl.loop(0, dx_ref.shape[0] // (2 * N_ACC))
    def _(i):
        for j in range(2 * N_ACC):
            pos = i * (2 * N_ACC) + j
            code = code_ref[0, 0, pos]
            acc = accs[j % N_ACC]
            row = pl.ds(code >> 2, 1)
            acc[row, :] += jnp.where(lane_group == (code & 3), wide_ref[pl.ds(pos, 1), :], 0.0)

    @pl.when(step == pl.num_programs(0) - 1)
    def _():
        size = accs[0].shape[0]

        @pl.loop(0, size // 128)
        def _(i):
            rows = pl.ds(pl.multiple_of(i * 128, 128), 128)
            total = accs[0][rows, :]
            for acc in accs[1:]:
                total = total + acc[rows, :]
            total = total.T
            for g in range(groups):
                out_ref[:, pl.ds(pl.multiple_of(g * size + i * 128, 128), 128)] = total[g * width:(g + 1) * width, :]


def codes(ids, padded, width, step):
    size = padded * width // 128
    group = (ids >= size).astype(jnp.int32) + (ids >= 2 * size).astype(jnp.int32) + (ids >= 3 * size).astype(jnp.int32)
    code = 4 * (ids - group * size) + group
    return code.reshape(ids.shape[0] // step, 1, step)


def lookup(code, table_t):
    width, padded = table_t.shape
    groups = 128 // width
    assert groups == 4
    size = padded // groups
    steps, _, step = code.shape
    table = jnp.concatenate([table_t[:, g * size:(g + 1) * size] for g in range(groups)], axis=0).astype(F32).T
    return pl.pallas_call(
        functools.partial(gather_kernel, width=width),
        grid=(steps,),
        in_specs=[pl.BlockSpec((1, 1, step), lambda i: (i, 0, 0), memory_space=pltpu.SMEM), pl.BlockSpec((size, 128), lambda i: (0, 0))],
        out_specs=pl.BlockSpec((step, width), lambda i: (i, 0)),
        out_shape=jax.ShapeDtypeStruct((steps * step, width), BF16),
        scratch_shapes=[pltpu.VMEM((step, 128), F32)],
        compiler_params=pltpu.CompilerParams(vmem_limit_bytes=32 * 1024 * 1024),
        name="lookup",
    )(code, table)


def lookup_grad(code, dx, padded):
    width = dx.shape[1]
    groups = 128 // width
    size = padded // groups
    steps, _, step = code.shape
    return pl.pallas_call(
        functools.partial(scatter_kernel, width=width),
        grid=(steps,),
        in_specs=[pl.BlockSpec((1, 1, step), lambda i: (i, 0, 0), memory_space=pltpu.SMEM), pl.BlockSpec((step, width), lambda i: (i, 0))],
        out_specs=pl.BlockSpec((width, padded), lambda i: (0, 0)),
        out_shape=jax.ShapeDtypeStruct((width, padded), F32),
        scratch_shapes=[pltpu.VMEM((step, 128), F32)] + [pltpu.VMEM((size, 128), F32)] * N_ACC,
        compiler_params=pltpu.CompilerParams(vmem_limit_bytes=63 * 1024 * 1024),
        name="lookup_grad",
    )(code, dx)


def adam_update(state, grad, decay):
    moment = BETA_ONE * state[1] + (1.0 - BETA_ONE) * grad
    second = BETA_TWO * state[2] + (1.0 - BETA_TWO) * grad * grad
    m_hat = moment / (1.0 - BETA_ONE ** ADAM_STEP)
    v_hat = second / (1.0 - BETA_TWO ** ADAM_STEP)
    master = state[0] * (1.0 - LEARN_RATE * decay) - LEARN_RATE * m_hat / (jnp.sqrt(v_hat) + ADAM_EPS)
    return jnp.stack([master, moment, second])


def as_rows(x):
    lead = x.shape[0]
    flat = x.reshape(lead, -1)
    size = flat.shape[1]
    total = -(-size // 2048) * 2048
    if total != size:
        flat = jnp.pad(flat, ((0, 0), (0, total - size)))
    return flat.reshape(lead, total // 128, 128)


def pack(parts):
    return jnp.concatenate([as_rows(x) for x in parts], axis=1)


def unpack(packed, shapes):
    out, at = [], 0
    lead = packed.shape[0]
    for shape in shapes:
        size = 1
        for s in shape:
            size *= s
        n_rows = -(-size // 2048) * 16
        piece = packed[:, at:at + n_rows, :].reshape(lead, n_rows * 128)
        out.append(piece[:, :size].reshape((lead,) + tuple(shape)))
        at += n_rows
    return out


def join(piece, axis):
    moved = jnp.moveaxis(piece, 0, axis)
    shape = moved.shape
    return moved.reshape(shape[:axis] + (shape[axis] * shape[axis + 1],) + shape[axis + 2:])


def split(full, axis, n_dev):
    shape = full.shape
    parts = full.reshape(shape[:axis] + (n_dev, shape[axis] // n_dev) + shape[axis + 1:])
    return jnp.moveaxis(parts, axis, 0)


def solution(mesh):
    n_dev = mesh.shape['dp']
    row_spec = P('dp', None)
    state_specs = (P(None, None, 'dp'), P(None, None, 'dp'), P(None, None, 'dp', None, None, None), P(None, None, None, None, 'dp'), P(None, None, 'dp', None), P(None, None, 'dp', None), P(None, None, 'dp'), P(None, None, 'dp'))

    def train_step(token_ids, target_ids, st_wte, st_wpe, st_qkv, st_proj, st_up, st_down, st_vec, st_lnf):
        num_layers = st_qkv.shape[1]
        n_heads, head_dim = st_proj.shape[2], st_proj.shape[3]
        batch_dev, seq_len = token_ids.shape
        vocab = st_wte.shape[1]
        pos_rows = st_wpe.shape[1]
        d_loc = st_wte.shape[2]
        d_model = d_loc * n_dev
        d_ff = st_up.shape[-1]
        n_tok = batch_dev * seq_len
        inv_tokens = 1.0 / (n_tok * n_dev)
        padded = -(-vocab // VOCAB_TILE) * VOCAB_TILE
        axes = (0, 1, 0, 0, 0)
        loc_shapes = ((d_loc, 3 * d_model), (d_model, d_loc), (d_loc, d_ff), (d_ff // n_dev, d_model), (st_vec.shape[2],))

        wte_s = jnp.swapaxes(st_wte, 1, 2)
        wte_t = jnp.pad(wte_s[0].astype(BF16), ((0, 0), (0, padded - vocab)))
        head_t = lax.all_gather(wte_t, 'dp', axis=0, tiled=True)

        pieces = []
        for layer in range(num_layers):
            for state, shape in zip((st_qkv, st_proj, st_up, st_down, st_vec), loc_shapes):
                pieces.append(state[0, layer].astype(BF16).reshape((1,) + shape))
        pieces.append(st_wpe[0, 2:2 + seq_len].astype(BF16)[None])
        pieces.append(st_lnf[0].astype(BF16)[None])
        gathered = lax.all_gather(pack(pieces)[0], 'dp', axis=0, tiled=False)
        full = unpack(gathered, loc_shapes * num_layers + ((seq_len, d_loc), (2, d_loc)))
        weights = []
        for layer in range(num_layers):
            weights.append(tuple(join(x, ax) for x, ax in zip(full[5 * layer:5 * layer + 5], axes)))
        wpe_c = join(full[5 * num_layers], 1)
        lnf_c = join(full[5 * num_layers + 1], 1)

        all_ids = lax.all_gather(token_ids.reshape(-1), 'dp', axis=0, tiled=True)
        code = codes(all_ids, padded, d_loc, 1024)
        found = lookup(code, wte_t)
        found = lax.all_to_all(found, 'dp', split_axis=0, concat_axis=1, tiled=True)
        residual = found.reshape(batch_dev, seq_len, d_model).astype(F32) + wpe_c.astype(F32)
        backs = []
        for layer in range(num_layers):
            residual, back = jax.vjp(functools.partial(block, n_heads=n_heads), residual, weights[layer])
            backs.append(back)
        normed, norm_back = jax.vjp(final_norm, residual, lnf_c)
        grad_head, loss_part, d_normed = head_loss(normed.reshape(n_tok, d_model), target_ids.reshape(n_tok), head_t, vocab, inv_tokens)
        head_loc = lax.psum_scatter(grad_head, 'dp', scatter_dimension=0, tiled=True)
        d_resid, d_lnf = norm_back(d_normed.reshape(residual.shape).astype(BF16))
        layer_loc = [None] * num_layers
        for layer in reversed(range(num_layers)):
            d_resid, d_w = backs[layer](d_resid)
            parts = [split(g.astype(F32), ax, n_dev) for g, ax in zip(d_w, axes)]
            shapes = list(loc_shapes)
            if layer == num_layers - 1:
                parts.append(split(d_lnf.astype(F32), 1, n_dev))
                shapes.append((2, d_loc))
            if layer == 0:
                parts.append(split(jnp.sum(d_resid, axis=0), 1, n_dev))
                shapes.append((seq_len, d_loc))
            summed = jnp.sum(lax.all_to_all(pack(parts), 'dp', split_axis=0, concat_axis=0, tiled=True), axis=0, keepdims=True)
            got = [x[0] for x in unpack(summed, shapes)]
            layer_loc[layer] = got[:5]
            if layer == num_layers - 1:
                lnf_g = got[5]
            if layer == 0:
                pos_g = got[-1]

        dx = lax.all_to_all(d_resid.reshape(n_tok, d_model), 'dp', split_axis=1, concat_axis=0, tiled=True)
        look = lookup_grad(code, dx, padded)
        grads = [(head_loc + look)[:, :vocab], jnp.pad(pos_g, ((2, pos_rows - 2 - seq_len), (0, 0)))]
        state_list = (st_qkv, st_proj, st_up, st_down, st_vec)
        for kind in range(5):
            grads.append(jnp.stack([layer_loc[layer][kind].reshape(state_list[kind].shape[2:]) for layer in range(num_layers)]))
        grads.append(lnf_g)
        local_sq = sum(jnp.sum(grad * grad) for grad in grads)
        sums = lax.psum(jnp.stack([local_sq, loss_part]), 'dp')
        grad_norm = jnp.sqrt(sums[0])
        clip_coef = jnp.minimum(1.0, CLIP_NORM / (grad_norm + 1e-6))
        states = (wte_s, st_wpe, st_qkv, st_proj, st_up, st_down, st_vec, st_lnf)
        new_states = tuple(adam_update(state, grad * clip_coef, decay) for state, grad, decay in zip(states, grads, DECAYS))
        return (sums[1], jnp.swapaxes(new_states[0], 1, 2)) + new_states[1:]

    return jax.shard_map(train_step, mesh=mesh, in_specs=(row_spec, row_spec) + state_specs, out_specs=(P(),) + state_specs, check_vma=False)
```

time: 2890 us -> 1380 us (0.48)
  matrix products: 1280 us -> 100 us
  Pallas kernels: 0 us -> 789 us
  other arithmetic: 772 us -> 145 us
  waiting for transfers between devices: 328 us -> 64.4 us
  blocking collectives: 274 us -> 38.1 us
    dot_general x52 -> x24, matrix products: 1200 us -> 100 us  [the longest x6 33.3 us: block(): jnp.einsum('bsd,dn->bsn', normed_in, qkv_w, preferred_element_type=F32)]
    pallas_call x0 -> x8, Pallas kernels: none -> 789 us  [the longest x1 322 us: head_loss(): pl.pallas_call(functools.partial(grad_kernel, tile=VOCAB_TILE, inv_tokens...]
    convert_element_type x20 -> x12, other arithmetic: 404 us -> 7.52 us  [the longest x1 2.1 us: train_step(): found.reshape(batch_dev, seq_len, d_model).astype(F32) + wpe_c.astype(F32)]
    unnamed x20 -> x3, waiting for transfers between devices: 311 us -> 0.05 us
    all_gather x9 -> x1, blocking collectives: 203 us -> 14.3 us  [train_step(): all_ids = lax.all_gather(token_ids.reshape(-1), 'dp', axis=0, tiled=True)]
    reduce_sum x26 -> x18, other arithmetic: 235 us -> 54 us  [the longest x10 29.3 us: layer_norm(): centered * lax.rsqrt(variance + NORM_EPS) * gain.astype(F32)]
    sub x2 -> x0, matrix products: 83.6 us -> none  [block(): attn_prob = jax.nn.softmax(scores, axis=-1).astype(jnp.bfloat16)]
    all_to_all x0 -> x4, waiting for transfers between devices: none -> 64.3 us  [the longest x1 35.9 us: train_step(): found = lax.all_to_all(found, 'dp', split_axis=0, concat_axis=1, tiled=True)]
  transfers between devices with their start and end apart: 13 -> 7, of which waited for: 3 -> 3; matrix products, arithmetic and copies ran while one was open for 9% -> 26% of each run, Pallas kernels for 0% -> 23%
where the time goes in v1:
time: 1380 us; the launch traced here: 1370 us
  Pallas kernels  789 us (57%)
  local copies, waits for them, and re-layouts  197 us (14%)
  other arithmetic  145 us (11%)
  matrix products  100 us (7%)
  waiting for transfers between devices  64.4 us (5%)
  blocking collectives  38.1 us (3%)
  between operations  22.9 us (2%)
    pallas_call x1, Pallas kernels, head_loss(): pl.pallas_call(functools.partial(grad_kernel, tile=VOCAB_TILE, inv_tokens...  322 us
    pallas_call x1, Pallas kernels, head_loss(): pl.pallas_call(functools.partial(lse_kernel, vocab=vocab, tile=VOCAB_TILE...  152 us
    pallas_call x2, Pallas kernels, block(): mixed = attention(qkv, n_heads)  118 us
    pallas_call x2, Pallas kernels, attn_fwd_call(): pl.pallas_call(functools.partial(attn_fwd_kernel, seq=seq, dm=dm, hd=dm /...  79 us
    pallas_call x1, Pallas kernels, lookup_grad(): pl.pallas_call(functools.partial(scatter_kernel, width=width), grid=(step...  71.1 us
    unnamed x383, local copies, waits for them, and re-layouts  54.2 us
    pallas_call x1, Pallas kernels, lookup(): pl.pallas_call(functools.partial(gather_kernel, width=width), grid=(steps...  46.6 us
    all_to_all x1, waiting for transfers between devices, train_step(): found = lax.all_to_all(found, 'dp', split_axis=0, concat_axis=1, tiled=True)  35.9 us
  transfers between devices with their start and end apart: 7, of which 3 were waited for; matrix products, arithmetic and copies ran while one was open for 26% of the time, Pallas kernels for 23%

profile of v1, /device:TPU:0, one launch (start us, length us, event | category | flops | bytes accessed | tf_op | source)
XLA Modules:
  0.0 1370.0 jit_solution(7809964459237798909)
XLA Ops:
  22.8 8.1 copy.118.table_ref
  30.9 14.3 %all_gather.9 = s32[24576]{0:T(1024)S(1)} all-gather(s32[3072]{0:T(1024)S(1)} %reshape.971), channel_id=1, replica_groups=mesh['dp'=8] {'dp'}, dimensions={0}, use_global_device_ids=true | all-gather | bytes 110592 | tf_op jit(solution)/shard_map/all_gather | solution.py:530
  48.1 46.6 %lookup.1 = bf16[24576,32]{1,0:T(8,128)(2,1)S(1)} custom-call(s32[24,1,1024]{2,1,0:T(1,128)S(1)} %bitcast.246, f32[12672,128]{1,0:T(8,128)S(1)} %copy-done), custom_call_target="tpu_custom_call" | custom-call | tf_op jit(solution)/shard_map/lookup/pallas_call | solution.py:414
  97.5 6.3 copy.119
  108.2 35.9 %all-to-all-done = bf16[8,3072,32]{1,2,0:T(8,128)(2,1)S(1)} async-done(((bf16[8,3072,32]{1,2,0:T(8,128)(2,1)}), bf16[8,3072,32]{1,2,0:T(8,128)(2,1)S(1)}, u32[]{:S(2)}, u32[]{:S(2)}) %all-to-all-start) | async-done | bytes 1572896 | tf_op jit(solution)/shard_map/all_to_all | solution.py:533
  146.3 5.3 reshape.1001
  166.4 3.6 add.416.clone
  170.1 5.4 add.418
  182.4 4.4 convert_element_type.577
  214.0 5.9 add_convert_fusion.1.qkv_ref
  219.9 39.6 %jvp_attn_fwd_.2 = (bf16[6,512,256]{2,1,0:T(8,128)(2,1)}, f32[6,16,512]{2,1,0:T(8,128)}) custom-call(bf16[6,512,768]{2,1,0:T(8,128)(2,1)} %add_convert_fusion.1.qkv_ref), custom_call_target="tpu_custom_call" | custom-call | flops 12884901888 | bytes 7077888 | tf_op jit(solution)/shard_map/jvp(attn_fwd)/pallas_call | solution.py:151
  263.3 4.0 fusion.37
  276.8 39.4 %jvp_attn_fwd_.3 = (bf16[6,512,256]{2,1,0:T(8,128)(2,1)}, f32[6,16,512]{2,1,0:T(8,128)}) custom-call(bf16[6,512,768]{2,1,0:T(8,128)(2,1)} %add_convert_fusion.qkv_ref), custom_call_target="tpu_custom_call" | custom-call | flops 12884901888 | bytes 7077888 | tf_op jit(solution)/shard_map/jvp(attn_fwd)/pallas_call | solution.py:151
  320.0 3.9 fusion.36
  332.9 152.1 %head_lse.1.lse_ref = f32[3072,1]{1,0:T(8,128)} custom-call(bf16[3072,256]{1,0:T(8,128)(2,1)} %bitcast.257, bf16[256,50688]{1,0:T(8,128)(2,1)} %all-gather.5.cloned.1.call-done.w_ref), custom_call_target="tpu_custom_call" | custom-call | flops 79725330432 | bytes 25952256 | tf_op jit(solution)/shard_map/head_lse/pallas_call | solution.py:322
  485.0 322.4 %head_grad.1 = (f32[1,3072,256]{2,1,0:T(8,128)}, f32[256,50688]{1,0:T(8,128)}, f32[1,3072,128]{2,1,0:T(8,128)}) custom-call(bf16[3072,256]{1,0:T(8,128)(2,1)} %bitcast.258, bf16[256,3072]{1,0:T(8,128)(2,1)} %bitcast.276, bf16[256,50688]{1,0:T(8,128)(2,1)} %all-gather.5.cloned.1.call-done.w_ref, f32[3072,1]{1,0:T(8,128)} %head_lse.1.lse_ref, s32[3072,1]{1,0:T(8,128)} %bitcast.275), custom_call_target="tpu_custom_call" | custom-call | flops 239175991296 | bytes 77856768 | tf_op jit(solution)/shard_map/head_grad/pallas_call | solution.py:333
  809.3 4.1 and_convert_fusion.1
  813.4 4.0 and_convert_fusion
  822.0 3.7 fusion.127
  829.8 3.7 fusion.30
  835.8 4.2 fusion.31
  846.7 59.0 %transpose_jvp_attn_bwd__.2 = bf16[6,512,768]{2,1,0:T(8,128)(2,1)} custom-call(bf16[6,512,768]{2,1,0:T(8,128)(2,1)} %add_convert_fusion.qkv_ref, bf16[6,512,256]{2,1,0:T(8,128)(2,1)} %fusion.147.do_ref, f32[6,16,512]{2,1,0:T(8,128)} %get-tuple-element.20.lse_ref), custom_call_target="tpu_custom_call" | custom-call | flops 32212254720 | bytes 14155776 | tf_op jit(solution)/shard_map/transpose(jvp(attn_bwd))/pallas_call | solution.py:204
  905.6 3.8 reduce_sum.534
  909.4 5.6 fusion.29
  917.8 4.1 fusion.32
  931.0 3.6 fusion.28
  937.0 4.3 fusion.33
  947.4 59.1 %transpose_jvp_attn_bwd__.3 = bf16[6,512,768]{2,1,0:T(8,128)(2,1)} custom-call(bf16[6,512,768]{2,1,0:T(8,128)(2,1)} %add_convert_fusion.1.qkv_ref, bf16[6,512,256]{2,1,0:T(8,128)(2,1)} %fusion.146.do_ref, f32[6,16,512]{2,1,0:T(8,128)} %get-tuple-element.21.lse_ref), custom_call_target="tpu_custom_call" | custom-call | flops 32212254720 | bytes 14155776 | tf_op jit(solution)/shard_map/transpose(jvp(attn_bwd))/pallas_call | solution.py:204
  1006.5 3.7 reduce_sum.517
  1010.2 6.5 fusion.27
  1020.1 5.3 fusion.34
  1025.4 6.0 fusion.124
  1031.4 5.2 copy.136
  1036.6 5.4 all_to_all.32
  1045.7 6.3 fusion.72
  1052.1 7.8 fusion.65
  1069.5 3.7 fusion.79
  1084.0 7.5 fusion.70
  1091.6 25.6 %all-to-all-done.1 = f32[3072,8,32]{0,2,1:T(8,128)} async-done(((f32[3072,8,32]{0,2,1:T(8,128)}), f32[3072,8,32]{0,2,1:T(8,128)}, u32[]{:S(2)}, u32[]{:S(2)}) %all-to-all-start.1) | async-done | bytes 3145760 | tf_op jit(solution)/shard_map/all_to_all | solution.py:562
  1123.0 7.0 fusion.64
  1138.4 5.5 fusion.74
  1179.0 8.4 copy.137
  1187.3 71.1 %lookup_grad.1 = f32[32,50688]{1,0:T(8,128)} custom-call(s32[24,1,1024]{2,1,0:T(1,128)} %bitcast.247, f32[24576,32]{1,0:T(8,128)} %bitcast.248), custom_call_target="tpu_custom_call" | custom-call | tf_op jit(solution)/shard_map/lookup_grad/pallas_call | solution.py:431
  1274.3 9.8 multiply_reduce_fusion
  1290.3 23.8 %psum.7 = f32[2]{0:T(128)S(1)} all-reduce(f32[2]{0:T(128)S(1)} %pad_maximum_fusion.7), channel_id=1, replica_groups=mesh['dp'=8] {'dp'}, use_global_device_ids=true, to_apply=%region_51.52 | all-reduce | flops 2 | bytes 16 | tf_op jit(solution)/shard_map/psum | solution.py:570
  1321.2 5.5 copy.161
  1332.5 14.5 %fusion.10 = (f32[1,32,50257]{2,1,0:T(8,128)S(1)}, f32[1,32,50257]{2,1,0:T(8,128)}, f32[1,32,50257]{2,1,0:T(8,128)}) fusion(f32[3,32,50257]{2,1,0:T(8,128)} %bitcast.250, f32[32,50257]{1,0:T(8,128)} %get-tuple-element.91, f32[]{:T(128)} %bitcast.51), kind=kLoop, calls=%fused_computation.28 | loop fusion | flops 22515136 | bytes 45030276 | tf_op jit(solution)/shard_map/stack | solution.py:449
  1353.3 9.7 maximum_bitcast_fusion
  (618 shorter events, 252.4 us)
Async XLA Ops:
  7.2 147.8 %all-gather.3.cloned.1.call-start = ((), (), s32[]{:S(2)}) async-start(), calls=%async_computation.5 | async-start | bytes 3944448 | tf_op jit(solution)/shard_map/all_gather | solution.py:522
  14.3 318.5 %all-gather.5.cloned.1.call-start = ((), (), s32[]{:S(2)}) async-start(), calls=%async_computation.6 | async-start | bytes 29196288 | tf_op jit(solution)/shard_map/all_gather | solution.py:514
  45.2 49.5 %copy-start.2 = (s32[24576]{0:T(1024)}, s32[24576]{0:T(1024)S(1)}, u32[]{:S(2)}) copy-start(s32[24576]{0:T(1024)S(1)} %multiply_add_fusion.4) | copy-start | bytes 294916
  103.8 40.4 %all-to-all-start = ((bf16[8,3072,32]{1,2,0:T(8,128)(2,1)}), bf16[8,3072,32]{1,2,0:T(8,128)(2,1)S(1)}, u32[]{:S(2)}, u32[]{:S(2)}) async-start(bf16[8,3072,32]{1,2,0:T(8,128)(2,1)} %copy.119), calls=%async_computation | async-start | bytes 3145728 | tf_op jit(solution)/shard_map/all_to_all | solution.py:533
  106.2 1168.1 %reduce-scatter.2.cloned.1.call-start = ((), (), s32[]{:S(2)}) async-start(), calls=%async_computation.7 | async-start | bytes 58392576 | tf_op jit(solution)/shard_map/reduce_scatter | solution.py:541
  155.0 104.6 %copy-start.12 = (f32[6,512,256]{2,1,0:T(8,128)}, f32[6,512,256]{2,1,0:T(8,128)S(1)}, u32[]{:S(2)}) copy-start(f32[6,512,256]{2,1,0:T(8,128)S(1)} %copy.125) | copy-start | bytes 9437188
  204.6 8.7 copy-start.122
  208.9 107.3 %copy-start.62 = (bf16[256,8,32]{0,2,1:T(8,128)(2,1)}, bf16[256,8,32]{0,2,1:T(8,128)(2,1)S(1)}, u32[]{:S(2)}) copy-start(bf16[256,8,32]{0,2,1:T(8,128)(2,1)S(1)} %copy.130) | copy-start | bytes 393220
  213.3 116.1 %copy-start.129 = (f32[256]{0:T(256)}, f32[256]{0:T(256)S(1)}, u32[]{:S(2)}) copy-start(f32[256]{0:T(256)S(1)} %reshape.1003) | copy-start | bytes 3076
  213.4 53.9 %copy-start.123 = (f32[1024]{0:T(1024)}, f32[1024]{0:T(1024)S(1)}, u32[]{:S(2)}) copy-start(f32[1024]{0:T(1024)S(1)} %slice_convert_fusion.7) | copy-start | bytes 12292
  213.4 110.6 %copy-start.125 = (f32[1024]{0:T(1024)}, f32[1024]{0:T(1024)S(1)}, u32[]{:S(2)}) copy-start(f32[1024]{0:T(1024)S(1)} %slice_convert_fusion.5) | copy-start | bytes 12292
  214.0 48.9 %copy-start.133 = (f32[256]{0:T(256)}, f32[256]{0:T(256)S(1)}, u32[]{:S(2)}) copy-start(f32[256]{0:T(256)S(1)} %get-tuple-element.150) | copy-start | bytes 3076
  214.0 48.9 %copy-start.152 = (f32[256]{0:T(256)}, f32[256]{0:T(256)S(1)}, u32[]{:S(2)}) copy-start(f32[256]{0:T(256)S(1)} %get-tuple-element.149) | copy-start | bytes 3076
  214.0 59.0 %copy-start.139 = (f32[256]{0:T(256)}, f32[256]{0:T(256)S(1)}, u32[]{:S(2)}) copy-start(f32[256]{0:T(256)S(1)} %get-tuple-element.157) | copy-start | bytes 3076
  214.0 59.0 %copy-start.156 = (f32[256]{0:T(256)}, f32[256]{0:T(256)S(1)}, u32[]{:S(2)}) copy-start(f32[256]{0:T(256)S(1)} %get-tuple-element.156) | copy-start | bytes 3076
  214.0 106.0 %copy-start.136 = (f32[256]{0:T(256)}, f32[256]{0:T(256)S(1)}, u32[]{:S(2)}) copy-start(f32[256]{0:T(256)S(1)} %get-tuple-element.154) | copy-start | bytes 3076
  214.0 106.0 %copy-start.154 = (f32[256]{0:T(256)}, f32[256]{0:T(256)S(1)}, u32[]{:S(2)}) copy-start(f32[256]{0:T(256)S(1)} %get-tuple-element.153) | copy-start | bytes 3076
  219.9 39.6 %copy-start.60 = (bf16[256,8,32]{0,2,1:T(8,128)(2,1)S(1)}, bf16[256,8,32]{0,2,1:T(8,128)(2,1)}, u32[]{:S(2)}) copy-start(bf16[256,8,32]{0,2,1:T(8,128)(2,1)} %copy.128) | copy-start | bytes 393220
  272.0 44.2 %copy-start.7 = (f32[6,512,256]{2,1,0:T(8,128)}, f32[6,512,256]{2,1,0:T(8,128)S(1)}, u32[]{:S(2)}) copy-start(f32[6,512,256]{2,1,0:T(8,128)S(1)} %get-tuple-element.165) | copy-start | bytes 9437188
  825.7 14.3 %copy-start.117 = (f32[6,512]{1,0:T(8,128)}, f32[6,512]{1,0:T(8,128)S(1)}, u32[]{:S(2)}) copy-start(f32[6,512]{1,0:T(8,128)S(1)} %negate_multiply_fusion.4) | copy-start | bytes 36868
  915.0 8.6 copy-start.166
  915.0 9.2 copy-start.102
  915.0 9.2 copy-start.140
  1020.1 11.3 copy-start.107
  1042.1 9.9 copy-start.91
  1042.1 9.9 copy-start.106
  1042.1 75.1 %all-to-all-start.1 = ((f32[3072,8,32]{0,2,1:T(8,128)}), f32[3072,8,32]{0,2,1:T(8,128)}, u32[]{:S(2)}, u32[]{:S(2)}) async-start(f32[3072,8,32]{0,2,1:T(8,128)} %all_to_all.32), calls=%async_computation.2 | async-start | bytes 6291456 | tf_op jit(solution)/shard_map/all_to_all | solution.py:562
  1045.7 14.2 %slice-start = ((s8[12582912]{0:T(1024)(128)(4,1)}), s8[4194304]{0:T(1024)(128)(4,1)S(1)}, s32[]{:S(2)}) async-start(s8[12582912]{0:T(1024)(128)(4,1)} %bitcast.253), calls=%async_computation.8 | async-start | bytes 8388608
  1045.7 14.2 %slice-start.1 = ((s8[12582912]{0:T(1024)(128)(4,1)}), s8[4194304]{0:T(1024)(128)(4,1)S(1)}, s32[]{:S(2)}) async-start(s8[12582912]{0:T(1024)(128)(4,1)} %bitcast.253), calls=%async_computation.9 | async-start | bytes 8388608
  1091.5 29.1 %copy-start.142 = (bf16[768]{0:T(1024)(128)(2,1)S(1)}, bf16[768]{0:T(1024)(128)(2,1)}, u32[]{:S(2)}) copy-start(bf16[768]{0:T(1024)(128)(2,1)} %reduce_sum.517) | copy-start | bytes 4612
  1091.5 29.1 %copy-start.145 = (bf16[256]{0:T(256)(128)(2,1)S(1)}, bf16[256]{0:T(256)(128)(2,1)}, u32[]{:S(2)}) copy-start(bf16[256]{0:T(256)(128)(2,1)} %get-tuple-element.86) | copy-start | bytes 1540
  1091.5 29.1 %copy-start.146 = (bf16[256]{0:T(256)(128)(2,1)S(1)}, bf16[256]{0:T(256)(128)(2,1)}, u32[]{:S(2)}) copy-start(bf16[256]{0:T(256)(128)(2,1)} %get-tuple-element.88) | copy-start | bytes 1540
  1091.5 29.1 %copy-start.149 = (bf16[1024]{0:T(1024)(128)(2,1)S(1)}, bf16[1024]{0:T(1024)(128)(2,1)}, u32[]{:S(2)}) copy-start(bf16[1024]{0:T(1024)(128)(2,1)} %get-tuple-element.182) | copy-start | bytes 6148
  1091.5 31.5 %copy-start.100 = (f32[6,512]{1,0:T(8,128)S(1)}, f32[6,512]{1,0:T(8,128)}, u32[]{:S(2)}) copy-start(f32[6,512]{1,0:T(8,128)} %copy-done.98) | copy-start | bytes 36868
  1091.6 31.5 %copy-start.135 = (f32[256]{0:T(256)S(1)}, f32[256]{0:T(256)}, u32[]{:S(2)}) copy-start(f32[256]{0:T(256)} %copy-done.133) | copy-start | bytes 3076
  1091.6 31.5 %copy-start.153 = (f32[256]{0:T(256)S(1)}, f32[256]{0:T(256)}, u32[]{:S(2)}) copy-start(f32[256]{0:T(256)} %copy-done.152) | copy-start | bytes 3076
  1117.2 42.6 %all-to-all-start.3 = ((f32[8,800,128]{2,1,0:T(8,128)}), f32[8,800,128]{2,1,0:T(8,128)}, u32[]{:S(2)}, u32[]{:S(2)}) async-start(f32[8,800,128]{2,1,0:T(8,128)} %concatenate.79), calls=%async_computation.4 | async-start | bytes 6553600 | tf_op jit(solution)/shard_map/all_to_all | solution.py:554
  1159.8 105.1 %all-to-all-start.2 = ((f32[8,912,128]{2,1,0:T(8,128)}), f32[8,912,128]{2,1,0:T(8,128)}, u32[]{:S(2)}, u32[]{:S(2)}) async-start(f32[8,912,128]{2,1,0:T(8,128)} %constant_dynamic-update-slice_fusion.12), calls=%async_computation.3 | async-start | bytes 7471104 | tf_op jit(solution)/shard_map/all_to_all | solution.py:554
  1274.3 41.2 %copy-start.144 = (f32[3,2,32]{2,1,0:T(2,128)S(1)}, f32[3,2,32]{2,1,0:T(2,128)}, u32[]{:S(2)}) copy-start(f32[3,2,32]{2,1,0:T(2,128)} %param.19) | copy-start | bytes 2308
  1274.3 41.2 %copy-start.38 = (f32[1,2,32,3,16,16]{5,4,3,2,1,0:T(8,128)S(1)}, f32[1,2,32,3,16,16]{5,4,3,2,1,0:T(8,128)}, u32[]{:S(2)}) copy-start(f32[1,2,32,3,16,16]{5,4,3,2,1,0:T(8,128)} %copy.181) | copy-start | bytes 589828
  1274.3 41.2 %copy-start.39 = (f32[1,2,32,3,16,16]{5,4,3,2,1,0:T(8,128)S(1)}, f32[1,2,32,3,16,16]{5,4,3,2,1,0:T(8,128)}, u32[]{:S(2)}) copy-start(f32[1,2,32,3,16,16]{5,4,3,2,1,0:T(8,128)} %copy.182) | copy-start | bytes 589828
  1332.4 14.6 %copy-start.120 = (f32[3,2,416]{2,1,0:T(2,128)S(1)}, f32[3,2,416]{2,1,0:T(2,128)}, u32[]{:S(2)}) copy-start(f32[3,2,416]{2,1,0:T(2,128)} %param.18) | copy-start | bytes 29956
  1332.4 14.6 %copy-start.49 = (f32[3,2,128,256]{3,2,1,0:T(8,128)S(1)}, f32[3,2,128,256]{3,2,1,0:T(8,128)}, u32[]{:S(2)}) copy-start(f32[3,2,128,256]{3,2,1,0:T(8,128)} %param.17) | copy-start | bytes 2359300
  1332.4 14.6 %copy-start.76 = (f32[1,1,128,256]{3,2,1,0:T(8,128)S(1)}, f32[1,1,128,256]{3,2,1,0:T(8,128)}, u32[]{:S(2)}) copy-start(f32[1,1,128,256]{3,2,1,0:T(8,128)} %stack.143) | copy-start | bytes 393220
  1332.4 14.6 %copy-start.78 = (f32[1,1,128,256]{3,2,1,0:T(8,128)S(1)}, f32[1,1,128,256]{3,2,1,0:T(8,128)}, u32[]{:S(2)}) copy-start(f32[1,1,128,256]{3,2,1,0:T(8,128)} %stack.142) | copy-start | bytes 393220
  1332.4 14.9 %copy-start.51 = (f32[3,2,32,1024]{3,2,1,0:T(8,128)S(1)}, f32[3,2,32,1024]{3,2,1,0:T(8,128)}, u32[]{:S(2)}) copy-start(f32[3,2,32,1024]{3,2,1,0:T(8,128)} %param.16) | copy-start | bytes 2359300
  1332.4 14.8 %copy-start.75 = (f32[1,1,32,1024]{3,2,1,0:T(8,128)S(1)}, f32[1,1,32,1024]{3,2,1,0:T(8,128)}, u32[]{:S(2)}) copy-start(f32[1,1,32,1024]{3,2,1,0:T(8,128)} %stack.139) | copy-start | bytes 393220
  1332.5 14.8 %copy-start.77 = (f32[1,1,32,1024]{3,2,1,0:T(8,128)S(1)}, f32[1,1,32,1024]{3,2,1,0:T(8,128)}, u32[]{:S(2)}) copy-start(f32[1,1,32,1024]{3,2,1,0:T(8,128)} %stack.138) | copy-start | bytes 393220
  (132 other events, 540.9 us)
Sparse Core Ops, SparseCore 0:
  14.5 31.3 all-gather.2
  47.6 139.9 all-gather.4
  807.6 314.1 reduce-scatter.1

commit v2 on v1

--- a/solution.py
+++ b/solution.py
@@ -15,14 +15,18 @@
 WEIGHT_DECAY = 0.1
 CLIP_NORM = 1.0
 ADAM_STEP = 10
-DECAYS = (WEIGHT_DECAY,) * 6 + (0.0, 0.0)
-VOCAB_TILE = 1536
+DECAYS = (WEIGHT_DECAY,) * 5 + (0.0, 0.0)
+LSE_TILE = 1536
+GRAD_TILE = 2304
+LCM_TILE = 4608
+ADAM_TILE = 4608
 TOKEN_TILE = 3072
 LSE_CHUNK = 128
 GRAD_CHUNK = 256
 N_ACC = 8
-HEADS_STEP = 2
+HEADS_STEP = 4
 LOWEST = -3.0e38
+FIRST = 0
 BIG_VMEM = 60 * 1024 * 1024
 F32 = jnp.float32
 BF16 = jnp.bfloat16
@@ -40,8 +44,8 @@
 
 
 def attn_fwd_kernel(qkv_ref, o_ref, lse_ref, qt_ref, vt_ref, ot_ref, *, seq, dm, hd):
-    qt_ref[...] = (qkv_ref[0, :, :dm] * jnp.asarray(hd ** -0.5, BF16)).T
-    vt_ref[...] = qkv_ref[0, :, 2 * dm:].T
+    qt_ref[...] = (qkv_ref[FIRST, :, :dm] * jnp.asarray(hd ** -0.5, BF16)).T
+    vt_ref[...] = qkv_ref[FIRST, :, 2 * dm:].T
     half = seq // 2
     per = 128 // hd
     lo, hi = slice(0, half), slice(half, seq)
@@ -56,8 +60,8 @@
             for j in range(HEADS_STEP):
                 hh = i * HEADS_STEP + j
                 qm = jnp.where(row_head == hh, qt_ref[base:base + 128, :], jnp.zeros((), BF16))
-                k_lo = qkv_ref[0, lo, dm + base:dm + base + 128]
-                k_hi = qkv_ref[0, hi, dm + base:dm + base + 128]
+                k_lo = qkv_ref[FIRST, lo, dm + base:dm + base + 128]
+                k_hi = qkv_ref[FIRST, hi, dm + base:dm + base + 128]
                 both = dot(k_lo, qm)
                 diag = dot(k_hi, qm[:, hi])
                 todo.append((hh, both[:, lo], both[:, hi], diag))
@@ -87,8 +91,8 @@
 
 def attn_bwd_kernel(qkv_ref, do_ref, lse_ref, dqkv_ref, qt_ref, kt_ref, dot_ref, dqt_ref, dk_ref, dv_ref, *, seq, dm, hd):
     scale = hd ** -0.5
-    qt_ref[...] = (qkv_ref[0, :, :dm] * jnp.asarray(scale, BF16)).T
-    kt_ref[...] = qkv_ref[0, :, dm:2 * dm].T
+    qt_ref[...] = (qkv_ref[FIRST, :, :dm] * jnp.asarray(scale, BF16)).T
+    kt_ref[...] = qkv_ref[FIRST, :, dm:2 * dm].T
     dot_ref[...] = do_ref[0].T
     dk_ref[...] = jnp.zeros_like(dk_ref)
     dv_ref[...] = jnp.zeros_like(dv_ref)
@@ -112,15 +116,15 @@
                 hh = i * HEADS_STEP + j
                 qm = jnp.where(row_head == hh, qt_ref[lanes, :], zero)
                 dom = jnp.where(row_head == hh, dot_ref[lanes, :], zero)
-                s_lo = dot(qkv_ref[0, lo, k_at], qm)
-                s_hi = dot(qkv_ref[0, hi, k_at], qm[:, hi])
-                dp_lo = dot(qkv_ref[0, lo, v_at], dom)
-                dp_hi = dot(qkv_ref[0, hi, v_at], dom[:, hi])
+                s_lo = dot(qkv_ref[FIRST, lo, k_at], qm)
+                s_hi = dot(qkv_ref[FIRST, hi, k_at], qm[:, hi])
+                dp_lo = dot(qkv_ref[FIRST, lo, v_at], dom)
+                dp_hi = dot(qkv_ref[FIRST, hi, v_at], dom[:, hi])
                 todo.append((hh, s_lo, s_hi, dp_lo, dp_hi))
             for hh, s_lo, s_hi, dp_lo, dp_hi in todo:
                 rows = pl.ds(pl.multiple_of(base + hh * hd, hd), hd)
                 lse = lse_ref[0, pl.ds(slab * per + hh, 1), :]
-                q_lane = jnp.where(lane_head == hh, qkv_ref[0, :, lanes], zero)
+                q_lane = jnp.where(lane_head == hh, qkv_ref[FIRST, :, lanes], zero)
                 do_lane = jnp.where(lane_head == hh, do_ref[0, :, lanes], zero)
                 p00 = jnp.exp(jnp.where(keep, s_lo[:, lo], -1e30) - lse[:, lo])
                 p01 = jnp.exp(s_lo[:, hi] - lse[:, hi])
@@ -139,9 +143,9 @@
                 dqt_ref[rows, lo] = dq[:, lo]
                 dqt_ref[rows, hi] = dq[:, hi] + dot(kt_ref[rows, hi], ds_hi)
 
-    dqkv_ref[0, :, :dm] = (dqt_ref[...] * scale).T.astype(BF16)
-    dqkv_ref[0, :, dm:2 * dm] = (dk_ref[...] * scale).astype(BF16)
-    dqkv_ref[0, :, 2 * dm:] = dv_ref[...].astype(BF16)
+    dqkv_ref[FIRST, :, :dm] = (dqt_ref[...] * scale).T.astype(BF16)
+    dqkv_ref[FIRST, :, dm:2 * dm] = (dk_ref[...] * scale).astype(BF16)
+    dqkv_ref[FIRST, :, 2 * dm:] = dv_ref[...].astype(BF16)
 
 
 def attn_fwd_call(qkv, n_heads):
@@ -313,16 +317,16 @@
 def head_loss(normed, target_ids, head_t, vocab, inv_tokens):
     n_tok, dm = normed.shape
     padded = head_t.shape[1]
-    n_v, n_t = padded // VOCAB_TILE, n_tok // TOKEN_TILE
+    n_t = n_tok // TOKEN_TILE
     flops = 2 * n_tok * padded * dm
     h_spec = pl.BlockSpec((TOKEN_TILE, dm), lambda v, t: (t, 0))
-    w_spec = pl.BlockSpec((dm, VOCAB_TILE), lambda v, t: (0, v))
+    w_spec = pl.BlockSpec((dm, GRAD_TILE), lambda v, t: (0, v))
     col_spec = pl.BlockSpec((TOKEN_TILE, 1), lambda v, t: (t, 0))
     full_col = pl.BlockSpec((n_tok, 1), lambda v, t: (0, 0))
     lse = pl.pallas_call(
-        functools.partial(lse_kernel, vocab=vocab, tile=VOCAB_TILE),
-        grid=(n_v, n_t),
-        in_specs=[h_spec, w_spec],
+        functools.partial(lse_kernel, vocab=vocab, tile=LSE_TILE),
+        grid=(padded // LSE_TILE, n_t),
+        in_specs=[h_spec, pl.BlockSpec((dm, LSE_TILE), lambda v, t: (0, v))],
         out_specs=full_col,
         out_shape=jax.ShapeDtypeStruct((n_tok, 1), F32),
         scratch_shapes=[pltpu.VMEM((n_t, TOKEN_TILE, 128), F32), pltpu.VMEM((n_t, TOKEN_TILE, 128), F32)],
@@ -331,12 +335,12 @@
         name="head_lse",
     )(normed, head_t)
     d_h, d_w, picked = pl.pallas_call(
-        functools.partial(grad_kernel, tile=VOCAB_TILE, inv_tokens=inv_tokens),
-        grid=(n_v, n_t),
+        functools.partial(grad_kernel, tile=GRAD_TILE, inv_tokens=inv_tokens),
+        grid=(padded // GRAD_TILE, n_t),
         in_specs=[h_spec, pl.BlockSpec((dm, TOKEN_TILE), lambda v, t: (0, t)), w_spec, col_spec, col_spec],
         out_specs=[pl.BlockSpec((n_t, TOKEN_TILE, dm), lambda v, t: (0, 0, 0)), w_spec, pl.BlockSpec((n_t, TOKEN_TILE, 128), lambda v, t: (0, 0, 0))],
         out_shape=[jax.ShapeDtypeStruct((n_t, TOKEN_TILE, dm), F32), jax.ShapeDtypeStruct((dm, padded), F32), jax.ShapeDtypeStruct((n_t, TOKEN_TILE, 128), F32)],
-        scratch_shapes=[pltpu.VMEM((VOCAB_TILE, dm), BF16), pltpu.VMEM((TOKEN_TILE, VOCAB_TILE), BF16)],
+        scratch_shapes=[pltpu.VMEM((GRAD_TILE, dm), BF16), pltpu.VMEM((TOKEN_TILE, GRAD_TILE), BF16)],
         compiler_params=pltpu.CompilerParams(vmem_limit_bytes=BIG_VMEM),
         cost_estimate=pl.CostEstimate(flops=3 * flops, bytes_accessed=head_t.size * 6, transcendentals=0),
         name="head_grad",
@@ -344,43 +348,35 @@
     return d_w, -jnp.sum(picked) * inv_tokens, d_h.reshape(n_tok, dm) * inv_tokens
 
 
-def gather_kernel(code_ref, table_ref, out_ref, wide_ref, *, width):
-    groups = 128 // width
-    lane_group = lax.broadcasted_iota(jnp.int32, (1, 128), 1) // width
-
+def gather_kernel(row_ref, mask_ref, table_ref, out_ref, wide_ref, *, width):
     @pl.loop(0, out_ref.shape[0] // 16)
     def _(i):
         for j in range(16):
             pos = i * 16 + j
-            code = code_ref[0, 0, pos]
-            row = table_ref[pl.ds(code >> 2, 1), :]
-            wide_ref[pl.ds(pos, 1), :] = jnp.where(lane_group == (code & 3), row, 0.0)
+            wide_ref[pl.ds(pos, 1), :] = table_ref[pl.ds(row_ref[0, 0, pos], 1), :]
 
     from_lane = lax.broadcasted_iota(jnp.int32, (128, width), 0) % width
     fold = (from_lane == lax.broadcasted_iota(jnp.int32, (128, width), 1)).astype(F32).astype(BF16)
-    out_ref[...] = dot(wide_ref[...].astype(BF16), fold).astype(BF16)
-
-
-def scatter_kernel(code_ref, dx_ref, out_ref, wide_ref, *accs, width):
+    out_ref[...] = dot(wide_ref[...].astype(BF16) * mask_ref[...], fold).astype(BF16)
+
+
+def scatter_kernel(row_ref, mask_ref, dx_ref, out_ref, wide_ref, *accs, width):
     step = pl.program_id(0)
     groups = 128 // width
-    lane_group = lax.broadcasted_iota(jnp.int32, (1, 128), 1) // width
 
     @pl.when(step == 0)
     def _():
         for acc in accs:
             acc[...] = jnp.zeros_like(acc)
 
-    wide_ref[...] = jnp.concatenate([dx_ref[...]] * groups, axis=1)
+    wide_ref[...] = jnp.concatenate([dx_ref[...]] * groups, axis=1) * mask_ref[...].astype(F32)
 
     @pl.loop(0, dx_ref.shape[0] // (2 * N_ACC))
     def _(i):
         for j in range(2 * N_ACC):
             pos = i * (2 * N_ACC) + j
-            code = code_ref[0, 0, pos]
             acc = accs[j % N_ACC]
-            row = pl.ds(code >> 2, 1)
-            acc[row, :] += jnp.where(lane_group == (code & 3), wide_ref[pl.ds(pos, 1), :], 0.0)
+            acc[pl.ds(row_ref[0, 0, pos], 1), :] += wide_ref[pl.ds(pos, 1), :]
 
     @pl.when(step == pl.num_programs(0) - 1)
     def _():
@@ -397,56 +393,121 @@
                 out_ref[:, pl.ds(pl.multiple_of(g * size + i * 128, 128), 128)] = total[g * width:(g + 1) * width, :]
 
 
-def codes(ids, padded, width, step):
+def places(ids, padded, width, step):
     size = padded * width // 128
     group = (ids >= size).astype(jnp.int32) + (ids >= 2 * size).astype(jnp.int32) + (ids >= 3 * size).astype(jnp.int32)
-    code = 4 * (ids - group * size) + group
-    return code.reshape(ids.shape[0] // step, 1, step)
-
-
-def lookup(code, table_t):
+    row = ids - group * size
+    mask = (group[:, None] == lax.broadcasted_iota(jnp.int32, (1, 128), 1) // width).astype(BF16)
+    return row.reshape(ids.shape[0] // step, 1, step), mask
+
+
+def lookup(row, mask, table_t):
     width, padded = table_t.shape
     groups = 128 // width
     assert groups == 4
     size = padded // groups
-    steps, _, step = code.shape
+    steps, _, step = row.shape
     table = jnp.concatenate([table_t[:, g * size:(g + 1) * size] for g in range(groups)], axis=0).astype(F32).T
     return pl.pallas_call(
         functools.partial(gather_kernel, width=width),
         grid=(steps,),
-        in_specs=[pl.BlockSpec((1, 1, step), lambda i: (i, 0, 0), memory_space=pltpu.SMEM), pl.BlockSpec((size, 128), lambda i: (0, 0))],
+        in_specs=[pl.BlockSpec((1, 1, step), lambda i: (i, 0, 0), memory_space=pltpu.SMEM), pl.BlockSpec((step, 128), lambda i: (i, 0)), pl.BlockSpec((size, 128), lambda i: (0, 0))],
         out_specs=pl.BlockSpec((step, width), lambda i: (i, 0)),
         out_shape=jax.ShapeDtypeStruct((steps * step, width), BF16),
         scratch_shapes=[pltpu.VMEM((step, 128), F32)],
         compiler_params=pltpu.CompilerParams(vmem_limit_bytes=32 * 1024 * 1024),
         name="lookup",
-    )(code, table)
-
-
-def lookup_grad(code, dx, padded):
+    )(row, mask, table)
+
+
+def lookup_grad(row, mask, dx, padded):
     width = dx.shape[1]
     groups = 128 // width
     size = padded // groups
-    steps, _, step = code.shape
+    steps, _, step = row.shape
     return pl.pallas_call(
         functools.partial(scatter_kernel, width=width),
         grid=(steps,),
-        in_specs=[pl.BlockSpec((1, 1, step), lambda i: (i, 0, 0), memory_space=pltpu.SMEM), pl.BlockSpec((step, width), lambda i: (i, 0))],
+        in_specs=[pl.BlockSpec((1, 1, step), lambda i: (i, 0, 0), memory_space=pltpu.SMEM), pl.BlockSpec((step, 128), lambda i: (i, 0)), pl.BlockSpec((step, width), lambda i: (i, 0))],
         out_specs=pl.BlockSpec((width, padded), lambda i: (0, 0)),
         out_shape=jax.ShapeDtypeStruct((width, padded), F32),
         scratch_shapes=[pltpu.VMEM((step, 128), F32)] + [pltpu.VMEM((size, 128), F32)] * N_ACC,
         compiler_params=pltpu.CompilerParams(vmem_limit_bytes=63 * 1024 * 1024),
+        cost_estimate=pl.CostEstimate(flops=60_000_000_000, bytes_accessed=0, transcendentals=0),
         name="lookup_grad",
-    )(code, dx)
-
-
-def adam_update(state, grad, decay):
-    moment = BETA_ONE * state[1] + (1.0 - BETA_ONE) * grad
-    second = BETA_TWO * state[2] + (1.0 - BETA_TWO) * grad * grad
+    )(row, mask, dx)
+
+
+def sum_kernel(x_ref, out_ref, got_ref, send_sem, recv_sem, *, n_dev):
+    me = lax.axis_index('dp')
+    barrier = pltpu.get_barrier_semaphore()
+    for k in range(1, n_dev):
+        pl.semaphore_signal(barrier, inc=1, device_id=(lax.rem(me + k, n_dev),), device_id_type=pl.DeviceIdType.MESH)
+    pl.semaphore_wait(barrier, n_dev - 1)
+    copies = []
+    for k in range(1, n_dev):
+        copy = pltpu.make_async_remote_copy(
+            src_ref=x_ref,
+            dst_ref=got_ref.at[me],
+            send_sem=send_sem.at[k - 1],
+            recv_sem=recv_sem.at[k - 1],
+            device_id=(lax.rem(me + k, n_dev),),
+            device_id_type=pl.DeviceIdType.MESH,
+        )
+        copy.start()
+        copies.append(copy)
+    got_ref[me] = x_ref[...]
+    for copy in copies:
+        copy.wait()
+    total = got_ref[0]
+    for k in range(1, n_dev):
+        total = total + got_ref[k]
+    out_ref[...] = total
+
+
+def device_sums(first, second, n_dev):
+    lane = lax.broadcasted_iota(jnp.int32, (8, 128), 1)
+    out = pl.pallas_call(
+        functools.partial(sum_kernel, n_dev=n_dev),
+        in_specs=[pl.BlockSpec(memory_space=pltpu.VMEM)],
+        out_specs=pl.BlockSpec(memory_space=pltpu.VMEM),
+        out_shape=jax.ShapeDtypeStruct((8, 128), F32),
+        scratch_shapes=[pltpu.VMEM((n_dev, 8, 128), F32), pltpu.SemaphoreType.DMA((n_dev - 1,)), pltpu.SemaphoreType.DMA((n_dev - 1,))],
+        compiler_params=pltpu.CompilerParams(collective_id=0, has_side_effects=True),
+        name="device_sums",
+    )(jnp.where(lane == 0, first, jnp.where(lane == 1, second, 0.0)))
+    return out[0, 0], out[0, 1]
+
+
+def adam_parts(master, moment, second, grad, decay):
+    moment = BETA_ONE * moment + (1.0 - BETA_ONE) * grad
+    second = BETA_TWO * second + (1.0 - BETA_TWO) * grad * grad
     m_hat = moment / (1.0 - BETA_ONE ** ADAM_STEP)
     v_hat = second / (1.0 - BETA_TWO ** ADAM_STEP)
-    master = state[0] * (1.0 - LEARN_RATE * decay) - LEARN_RATE * m_hat / (jnp.sqrt(v_hat) + ADAM_EPS)
-    return jnp.stack([master, moment, second])
+    return master * (1.0 - LEARN_RATE * decay) - LEARN_RATE * m_hat / (jnp.sqrt(v_hat) + ADAM_EPS), moment, second
+
+
+def adam_update(state, grad, decay):
+    return jnp.stack(adam_parts(*state, grad, decay))
+
+
+def adam_kernel(clip_ref, state_ref, head_ref, look_ref, out_ref):
+    grad = (head_ref[...] + look_ref[...]) * clip_ref[0]
+    out_ref[...] = jnp.stack(adam_parts(*state_ref[...], grad, WEIGHT_DECAY))
+
+
+def adam_table(state, head, look, clip_coef):
+    kinds, width, vocab = state.shape
+    state_spec = pl.BlockSpec((kinds, width, ADAM_TILE), lambda i: (0, 0, i))
+    grad_spec = pl.BlockSpec((width, ADAM_TILE), lambda i: (0, i))
+    return pl.pallas_call(
+        adam_kernel,
+        grid=(pl.cdiv(vocab, ADAM_TILE),),
+        in_specs=[pl.BlockSpec(memory_space=pltpu.SMEM), state_spec, grad_spec, grad_spec],
+        out_specs=state_spec,
+        out_shape=jax.ShapeDtypeStruct(state.shape, F32),
+        name="adam_table",
+    )(clip_coef.reshape(1), state, head, look)
 
 
 def as_rows(x):
@@ -492,7 +553,7 @@
 def solution(mesh):
     n_dev = mesh.shape['dp']
     row_spec = P('dp', None)
-    state_specs = (P(None, None, 'dp'), P(None, None, 'dp'), P(None, None, 'dp', None, None, None), P(None, None, None, None, 'dp'), P(None, None, 'dp', None), P(None, None, 'dp', None), P(None, None, 'dp'), P(None, None, 'dp'))
+    state_specs = tuple(P(*(lead * (None,)), 'dp') for lead in (2, 2, 2, 4, 2, 2, 2, 2))
 
     def train_step(token_ids, target_ids, st_wte, st_wpe, st_qkv, st_proj, st_up, st_down, st_vec, st_lnf):
         num_layers = st_qkv.shape[1]
@@ -505,13 +566,12 @@
         d_ff = st_up.shape[-1]
         n_tok = batch_dev * seq_len
         inv_tokens = 1.0 / (n_tok * n_dev)
-        padded = -(-vocab // VOCAB_TILE) * VOCAB_TILE
+        padded = -(-vocab // LCM_TILE) * LCM_TILE
         axes = (0, 1, 0, 0, 0)
         loc_shapes = ((d_loc, 3 * d_model), (d_model, d_loc), (d_loc, d_ff), (d_ff // n_dev, d_model), (st_vec.shape[2],))
 
         wte_s = jnp.swapaxes(st_wte, 1, 2)
         wte_t = jnp.pad(wte_s[0].astype(BF16), ((0, 0), (0, padded - vocab)))
-        head_t = lax.all_gather(wte_t, 'dp', axis=0, tiled=True)
 
         pieces = []
         for layer in range(num_layers):
@@ -528,9 +588,11 @@
         lnf_c = join(full[5 * num_layers + 1], 1)
 
         all_ids = lax.all_gather(token_ids.reshape(-1), 'dp', axis=0, tiled=True)
-        code = codes(all_ids, padded, d_loc, 1024)
-        found = lookup(code, wte_t)
+        row, mask = places(all_ids, padded, d_loc, 1024)
+        found = lookup(row, mask, wte_t)
         found = lax.all_to_all(found, 'dp', split_axis=0, concat_axis=1, tiled=True)
+        wte_late, found = lax.optimization_barrier((wte_t, found))
+        head_t = lax.all_gather(wte_late, 'dp', axis=0, tiled=True)
         residual = found.reshape(batch_dev, seq_len, d_model).astype(F32) + wpe_c.astype(F32)
         backs = []
         for layer in range(num_layers):
@@ -541,6 +603,7 @@
         head_loc = lax.psum_scatter(grad_head, 'dp', scatter_dimension=0, tiled=True)
         d_resid, d_lnf = norm_back(d_normed.reshape(residual.shape).astype(BF16))
         layer_loc = [None] * num_layers
+        swapped, all_shapes = [], []
         for layer in reversed(range(num_layers)):
             d_resid, d_w = backs[layer](d_resid)
             parts = [split(g.astype(F32), ax, n_dev) for g, ax in zip(d_w, axes)]
@@ -551,27 +614,37 @@
             if layer == 0:
                 parts.append(split(jnp.sum(d_resid, axis=0), 1, n_dev))
                 shapes.append((seq_len, d_loc))
-            summed = jnp.sum(lax.all_to_all(pack(parts), 'dp', split_axis=0, concat_axis=0, tiled=True), axis=0, keepdims=True)
-            got = [x[0] for x in unpack(summed, shapes)]
+            packed = pack(parts)
+            all_shapes.append(shapes)
+            if layer > 0:
+                packed, d_resid = lax.optimization_barrier((packed, d_resid))
+                swapped.append(lax.all_to_all(packed, 'dp', split_axis=0, concat_axis=0, tiled=True))
+
+
+        d_resid, swapped[0] = lax.optimization_barrier((d_resid, swapped[0]))
+        dx = lax.all_to_all(d_resid.reshape(n_tok, d_model), 'dp', split_axis=1, concat_axis=0, tiled=True)
+        packed, dx = lax.optimization_barrier((packed, dx))
+        swapped.append(lax.all_to_all(packed, 'dp', split_axis=0, concat_axis=0, tiled=True))
+        for layer, pieces_in, shapes in zip(reversed(range(num_layers)), swapped, all_shapes):
+            got = [x[0] for x in unpack(jnp.sum(pieces_in, axis=0, keepdims=True), shapes)]
             layer_loc[layer] = got[:5]
             if layer == num_layers - 1:
                 lnf_g = got[5]
             if layer == 0:
                 pos_g = got[-1]
-
-        dx = lax.all_to_all(d_resid.reshape(n_tok, d_model), 'dp', split_axis=1, concat_axis=0, tiled=True)
-        look = lookup_grad(code, dx, padded)
+        look = lookup_grad(row, mask, dx, padded)
         grads = [(head_loc + look)[:, :vocab], jnp.pad(pos_g, ((2, pos_rows - 2 - seq_len), (0, 0)))]
         state_list = (st_qkv, st_proj, st_up, st_down, st_vec)
         for kind in range(5):
             grads.append(jnp.stack([layer_loc[layer][kind].reshape(state_list[kind].shape[2:]) for layer in range(num_layers)]))
         grads.append(lnf_g)
         local_sq = sum(jnp.sum(grad * grad) for grad in grads)
-        sums = lax.psum(jnp.stack([local_sq, loss_part]), 'dp')
-        grad_norm = jnp.sqrt(sums[0])
+        total_sq, loss = device_sums(local_sq, loss_part, n_dev)
+        grad_norm = jnp.sqrt(total_sq)
         clip_coef = jnp.minimum(1.0, CLIP_NORM / (grad_norm + 1e-6))
-        states = (wte_s, st_wpe, st_qkv, st_proj, st_up, st_down, st_vec, st_lnf)
-        new_states = tuple(adam_update(state, grad * clip_coef, decay) for state, grad, decay in zip(states, grads, DECAYS))
-        return (sums[1], jnp.swapaxes(new_states[0], 1, 2)) + new_states[1:]
+        new_wte = adam_table(wte_s, head_loc, look, clip_coef)
+        states = (st_wpe, st_qkv, st_proj, st_up, st_down, st_vec, st_lnf)
+        new_states = tuple(adam_update(state, grad * clip_coef, decay) for state, grad, decay in zip(states, grads[1:], DECAYS))
+        return (loss, jnp.swapaxes(new_wte, 1, 2)) + new_states
 
     return jax.shard_map(train_step, mesh=mesh, in_specs=(row_spec, row_spec) + state_specs, out_specs=(P(),) + state_specs, check_vma=False)

time: 1380 us -> 1260 us (0.913)
  waiting for transfers between devices: 64.4 us -> 27.3 us
  Pallas kernels: 789 us -> 759 us
  blocking collectives: 38.1 us -> 14.7 us
  other arithmetic: 145 us -> 131 us
    psum x1 -> x0, blocking collectives: 23.8 us -> none  [train_step(): sums = lax.psum(jnp.stack([local_sq, loss_part]), 'dp')]
    pallas_call x2 -> x4, Pallas kernels: 475 us -> 492 us  [the longest x1 312 us: head_loss(): pl.pallas_call(functools.partial(grad_kernel, tile=GRAD_TILE, inv_tokens=...]
    all_to_all x1, waiting for transfers between devices: 25.6 us -> 8.25 us  [train_step(): lax.all_to_all(d_resid.reshape(n_tok, d_model), 'dp', split_axis=1, conca...]
    all_to_all x1, waiting for transfers between devices: 35.9 us -> 19 us  [train_step(): found = lax.all_to_all(found, 'dp', split_axis=0, concat_axis=1, tiled=True)]
    another operation x15 -> x13, other arithmetic: 26.3 us -> 11.7 us  [the longest x8 9.6 us: adam_update(): return jnp.stack(adam_parts(*state, grad, decay))]
    pallas_call x1, Pallas kernels: 46.6 us -> 32.3 us  [lookup(): pl.pallas_call(functools.partial(gather_kernel, width=width), grid=(steps...]
    pallas_call x2, Pallas kernels: 79 us -> 65 us  [attn_fwd_call(): pl.pallas_call(functools.partial(attn_fwd_kernel, seq=seq, dm=dm, hd=dm /...]
    reduce_sum x10 -> x8, other arithmetic: 29.3 us -> 17.2 us  [layer_norm(): centered * lax.rsqrt(variance + NORM_EPS) * gain.astype(F32)]
  transfers between devices with their start and end apart: 7 -> 7, of which waited for: 3 -> 2; matrix products, arithmetic and copies ran while one was open for 26% -> 28% of each run, Pallas kernels for 23% -> 21%
where the time goes in v2:
time: 1260 us
  Pallas kernels  759 us (60%)
  local copies, waits for them, and re-layouts  185 us (15%)
  other arithmetic  131 us (10%)
  matrix products  103 us (8%)
  waiting for transfers between devices  27.3 us (2%)
  between operations  22.7 us (2%)
  blocking collectives  14.7 us (1%)
  starting transfers between devices  13.6 us (1%)
    pallas_call x1, Pallas kernels, head_loss(): pl.pallas_call(functools.partial(grad_kernel, tile=GRAD_TILE, inv_tokens=...  312 us
    pallas_call x1, Pallas kernels, head_loss(): pl.pallas_call(functools.partial(lse_kernel, vocab=vocab, tile=LSE_TILE),...  152 us
    pallas_call x2, Pallas kernels, block(): mixed = attention(qkv, n_heads)  112 us
    pallas_call x2, Pallas kernels, attn_fwd_call(): pl.pallas_call(functools.partial(attn_fwd_kernel, seq=seq, dm=dm, hd=dm /...  65 us
    pallas_call x1, Pallas kernels, lookup_grad(): pl.pallas_call(functools.partial(scatter_kernel, width=width), grid=(step...  57.6 us
    unnamed x371, local copies, waits for them, and re-layouts  48.6 us
    pallas_call x1, Pallas kernels, lookup(): pl.pallas_call(functools.partial(gather_kernel, width=width), grid=(steps...  32.3 us
    dot_general x6, matrix products, block(): jnp.einsum('bsf,fd->bsd', hidden, down_w, preferred_element_type=F32)  30 us
  transfers between devices with their start and end apart: 7, of which 2 were waited for; matrix products, arithmetic and copies ran while one was open for 28% of the time, Pallas kernels for 21%

profile of v2, /device:TPU:0, one launch (start us, length us, event | category | flops | bytes accessed | tf_op | source)
XLA Modules:
  0.0 1256.0 jit_solution(14188577347000018722)
XLA Ops:
  20.7 8.1 copy.115.table_ref
  28.8 14.7 %all_gather.9 = s32[24576]{0:T(1024)S(1)} all-gather(s32[3072]{0:T(1024)S(1)} %reshape.996), channel_id=1, replica_groups=mesh['dp'=8] {'dp'}, dimensions={0}, use_global_device_ids=true | all-gather | bytes 110592 | tf_op jit(solution)/shard_map/all_gather | solution.py:590
  43.5 11.0 compare_convert_fusion.mask_ref
  54.6 32.3 %lookup.1 = bf16[24576,32]{1,0:T(8,128)(2,1)S(1)} custom-call(s32[24,1,1024]{2,1,0:T(1,128)S(1)} %bitcast.209, bf16[24576,128]{1,0:T(8,128)(2,1)S(1)} %compare_convert_fusion.mask_ref, f32[12672,128]{1,0:T(8,128)S(1)} %copy-done), custom_call_target="tpu_custom_call" | custom-call | tf_op jit(solution)/shard_map/lookup/pallas_call | solution.py:411
  89.6 6.3 copy.116
  100.9 19.0 %all-to-all-done = bf16[8,3072,32]{1,2,0:T(8,128)(2,1)} async-done(((bf16[8,3072,32]{1,2,0:T(8,128)(2,1)}), bf16[8,3072,32]{1,2,0:T(8,128)(2,1)}, u32[]{:S(2)}, u32[]{:S(2)}) %all-to-all-start) | async-done | bytes 1572896 | tf_op jit(solution)/shard_map/all_to_all | solution.py:593
  136.2 3.6 copy.123
  147.6 3.4 add_convert_fusion.7
  180.3 5.0 add_convert_fusion.1.qkv_ref
  185.3 32.5 %jvp_attn_fwd_.2 = (bf16[6,512,256]{2,1,0:T(8,128)(2,1)}, f32[6,16,512]{2,1,0:T(8,128)}) custom-call(bf16[6,512,768]{2,1,0:T(8,128)(2,1)} %add_convert_fusion.1.qkv_ref), custom_call_target="tpu_custom_call" | custom-call | flops 12884901888 | bytes 7077888 | tf_op jit(solution)/shard_map/jvp(attn_fwd)/pallas_call | solution.py:155
  221.6 4.0 fusion.34
  231.6 3.4 add_convert_fusion.qkv_ref
  235.0 32.6 %jvp_attn_fwd_.3 = (bf16[6,512,256]{2,1,0:T(8,128)(2,1)}, f32[6,16,512]{2,1,0:T(8,128)}) custom-call(bf16[6,512,768]{2,1,0:T(8,128)(2,1)} %add_convert_fusion.qkv_ref), custom_call_target="tpu_custom_call" | custom-call | flops 12884901888 | bytes 7077888 | tf_op jit(solution)/shard_map/jvp(attn_fwd)/pallas_call | solution.py:155
  271.4 4.0 fusion.33
  284.4 152.1 %head_lse.1.lse_ref = f32[3072,1]{1,0:T(8,128)} custom-call(bf16[3072,256]{1,0:T(8,128)(2,1)} %bitcast.225, bf16[256,50688]{1,0:T(8,128)(2,1)} %all-gather.5.cloned.1.call-done.w_ref), custom_call_target="tpu_custom_call" | custom-call | flops 79725330432 | bytes 25952256 | tf_op jit(solution)/shard_map/head_lse/pallas_call | solution.py:326
  436.5 311.8 %head_grad.1 = (f32[1,3072,256]{2,1,0:T(8,128)}, f32[256,50688]{1,0:T(8,128)}, f32[1,3072,128]{2,1,0:T(8,128)}) custom-call(bf16[3072,256]{1,0:T(8,128)(2,1)} %bitcast.226, bf16[256,3072]{1,0:T(8,128)(2,1)} %bitcast.244, bf16[256,50688]{1,0:T(8,128)(2,1)} %all-gather.5.cloned.1.call-done.w_ref, f32[3072,1]{1,0:T(8,128)} %head_lse.1.lse_ref, s32[3072,1]{1,0:T(8,128)} %bitcast.242), custom_call_target="tpu_custom_call" | custom-call | flops 239175991296 | bytes 77856768 | tf_op jit(solution)/shard_map/head_grad/pallas_call | solution.py:337
  764.7 4.1 and_convert_fusion.1
  768.9 4.0 and_convert_fusion
  777.4 3.7 fusion.119
  785.1 3.9 fusion.27
  791.4 4.2 fusion.28
  802.3 56.0 %transpose_jvp_attn_bwd__.2 = bf16[6,512,768]{2,1,0:T(8,128)(2,1)} custom-call(bf16[6,512,768]{2,1,0:T(8,128)(2,1)} %add_convert_fusion.qkv_ref, bf16[6,512,256]{2,1,0:T(8,128)(2,1)} %fusion.139.do_ref, f32[6,16,512]{2,1,0:T(8,128)} %get-tuple-element.30.lse_ref), custom_call_target="tpu_custom_call" | custom-call | flops 32212254720 | bytes 14155776 | tf_op jit(solution)/shard_map/transpose(jvp(attn_bwd))/pallas_call | solution.py:208
  858.3 3.8 reduce_sum.504
  862.1 5.5 fusion.26
  870.3 4.4 fusion.71
  875.6 8.6 fusion.61
  886.2 8.1 fusion.60
  902.5 5.2 fusion.67
  915.8 3.3 add_add_fusion.7
  919.1 3.6 all-to-all-start.1
  922.8 5.1 fusion
  939.5 56.0 %transpose_jvp_attn_bwd__.3 = bf16[6,512,768]{2,1,0:T(8,128)(2,1)} custom-call(bf16[6,512,768]{2,1,0:T(8,128)(2,1)} %add_convert_fusion.1.qkv_ref, bf16[6,512,256]{2,1,0:T(8,128)(2,1)} %fusion.138.do_ref, f32[6,16,512]{2,1,0:T(8,128)} %get-tuple-element.32.lse_ref), custom_call_target="tpu_custom_call" | custom-call | flops 32212254720 | bytes 14155776 | tf_op jit(solution)/shard_map/transpose(jvp(attn_bwd))/pallas_call | solution.py:208
  995.6 5.0 fusion.24
  1010.8 7.0 fusion.115
  1025.7 8.3 fusion.65
  1036.3 7.0 fusion.59
  1045.7 5.2 copy.147
  1050.8 5.4 all_to_all.39
  1059.4 3.2 fusion.74
  1065.4 5.5 fusion.69
  1089.0 8.2 all-to-all-done.2
  1097.2 8.4 copy.148
  1105.6 3.5 all-to-all-start.3
  1109.1 57.6 %lookup_grad.1.look_ref = f32[32,50688]{1,0:T(8,128)} custom-call(s32[24,1,1024]{2,1,0:T(1,128)} %bitcast.210, bf16[24576,128]{1,0:T(8,128)(2,1)} %copy-done.1, f32[24576,32]{1,0:T(8,128)} %bitcast.222), custom_call_target="tpu_custom_call" | custom-call | flops 60000002048 | tf_op jit(solution)/shard_map/lookup_grad/pallas_call | solution.py:428
  1177.9 7.1 fusion.7
  1190.6 6.5 device_sums.1
  1205.6 5.8 copy.158
  1227.7 21.5 %adam_table.1 = f32[3,32,50257]{2,1,0:T(8,128)} custom-call(f32[1]{0:T(128)} %bitcast.51.clip_ref, f32[3,32,50257]{2,1,0:T(8,128)} %bitcast.217, f32[32,50688]{1,0:T(8,128)} %reduce-scatter.2.cloned.1.call-done.head_ref, f32[32,50688]{1,0:T(8,128)} %lookup_grad.1.look_ref), custom_call_target="tpu_custom_call" | custom-call | tf_op jit(solution)/shard_map/adam_table/pallas_call | solution.py:503
  (604 shorter events, 245.0 us)
Async XLA Ops:
  7.2 116.3 %all-gather.3.cloned.1.call-start = ((), (), s32[]{:S(2)}) async-start(), calls=%async_computation.5 | async-start | bytes 3944448 | tf_op jit(solution)/shard_map/all_gather | solution.py:582
  20.7 8.1 copy-start.127
  43.5 11.1 copy-start
  43.5 11.0 copy-start.3
  54.6 32.3 %copy-start.1 = (bf16[24576,128]{1,0:T(8,128)(2,1)}, bf16[24576,128]{1,0:T(8,128)(2,1)S(1)}, u32[]{:S(2)}) copy-start(bf16[24576,128]{1,0:T(8,128)(2,1)S(1)} %compare_convert_fusion.mask_ref) | copy-start | bytes 18874372
  95.9 23.9 %all-to-all-start = ((bf16[8,3072,32]{1,2,0:T(8,128)(2,1)}), bf16[8,3072,32]{1,2,0:T(8,128)(2,1)}, u32[]{:S(2)}, u32[]{:S(2)}) async-start(bf16[8,3072,32]{1,2,0:T(8,128)(2,1)} %copy.116), calls=%async_computation | async-start | bytes 3145728 | tf_op jit(solution)/shard_map/all_to_all | solution.py:593
  98.9 185.4 %all-gather.5.cloned.1.call-start = ((), (), s32[]{:S(2)}) async-start(), calls=%async_computation.6 | async-start | bytes 29196288 | tf_op jit(solution)/shard_map/all_gather | solution.py:595
  100.9 19.2 %copy-start.128 = (s32[6,512]{1,0:T(8,128)S(1)}, s32[6,512]{1,0:T(8,128)}, u32[]{:S(2)}) copy-start(s32[6,512]{1,0:T(8,128)} %param.11) | copy-start | bytes 36868
  119.8 1058.0 %reduce-scatter.2.cloned.1.call-start = ((), (), s32[]{:S(2)}) async-start(), calls=%async_computation.7 | async-start | bytes 58392576 | tf_op jit(solution)/shard_map/reduce_scatter | solution.py:603
  123.5 94.3 %copy-start.12 = (f32[3072,256]{1,0:T(8,128)}, f32[3072,256]{1,0:T(8,128)S(1)}, u32[]{:S(2)}) copy-start(f32[3072,256]{1,0:T(8,128)S(1)} %copy.117) | copy-start | bytes 9437188
  171.5 8.7 copy-start.119
  175.8 91.8 %copy-start.57 = (bf16[256,8,32]{0,2,1:T(8,128)(2,1)}, bf16[256,8,32]{0,2,1:T(8,128)(2,1)S(1)}, u32[]{:S(2)}) copy-start(bf16[256,8,32]{0,2,1:T(8,128)(2,1)S(1)} %copy.127) | copy-start | bytes 393220
  180.2 100.7 %copy-start.129 = (f32[256]{0:T(256)}, f32[256]{0:T(256)S(1)}, u32[]{:S(2)}) copy-start(f32[256]{0:T(256)S(1)} %reshape.1029) | copy-start | bytes 3076
  180.2 45.3 %copy-start.123 = (f32[1024]{0:T(1024)}, f32[1024]{0:T(1024)S(1)}, u32[]{:S(2)}) copy-start(f32[1024]{0:T(1024)S(1)} %slice_convert_fusion.7) | copy-start | bytes 12292
  180.3 95.2 %copy-start.125 = (f32[1024]{0:T(1024)}, f32[1024]{0:T(1024)S(1)}, u32[]{:S(2)}) copy-start(f32[1024]{0:T(1024)S(1)} %slice_convert_fusion.5) | copy-start | bytes 12292
  180.3 51.0 %copy-start.134 = (f32[256]{0:T(256)}, f32[256]{0:T(256)S(1)}, u32[]{:S(2)}) copy-start(f32[256]{0:T(256)S(1)} %get-tuple-element.161) | copy-start | bytes 3076
  180.3 51.0 %copy-start.157 = (f32[256]{0:T(256)}, f32[256]{0:T(256)S(1)}, u32[]{:S(2)}) copy-start(f32[256]{0:T(256)S(1)} %get-tuple-element.160) | copy-start | bytes 3076
  180.3 91.1 %copy-start.137 = (f32[256]{0:T(256)}, f32[256]{0:T(256)S(1)}, u32[]{:S(2)}) copy-start(f32[256]{0:T(256)S(1)} %get-tuple-element.158) | copy-start | bytes 3076
  180.3 91.1 %copy-start.159 = (f32[256]{0:T(256)}, f32[256]{0:T(256)S(1)}, u32[]{:S(2)}) copy-start(f32[256]{0:T(256)S(1)} %get-tuple-element.157) | copy-start | bytes 3076
  185.3 32.5 %copy-start.55 = (bf16[256,8,32]{0,2,1:T(8,128)(2,1)S(1)}, bf16[256,8,32]{0,2,1:T(8,128)(2,1)}, u32[]{:S(2)}) copy-start(bf16[256,8,32]{0,2,1:T(8,128)(2,1)} %copy.125) | copy-start | bytes 393220
  185.3 32.5 %copy-start.144 = (f32[256]{0:T(256)S(1)}, f32[256]{0:T(256)}, u32[]{:S(2)}) copy-start(f32[256]{0:T(256)} %get-tuple-element.165) | copy-start | bytes 3076
  230.3 37.3 %copy-start.8 = (f32[6,512,256]{2,1,0:T(8,128)}, f32[6,512,256]{2,1,0:T(8,128)S(1)}, u32[]{:S(2)}) copy-start(f32[6,512,256]{2,1,0:T(8,128)S(1)} %get-tuple-element.175) | copy-start | bytes 9437188
  760.3 8.6 copy-start.64
  764.7 8.2 copy-start.42
  781.1 14.6 %copy-start.113 = (f32[6,512]{1,0:T(8,128)}, f32[6,512]{1,0:T(8,128)S(1)}, u32[]{:S(2)}) copy-start(f32[6,512]{1,0:T(8,128)S(1)} %negate_multiply_fusion.4) | copy-start | bytes 36868
  867.6 7.9 copy-start.114
  867.6 7.9 copy-start.126
  875.5 10.7 copy-start.86
  875.5 10.7 copy-start.103
  875.5 10.7 copy-start.139
  875.5 10.6 copy-start.160
  919.1 126.6 %all-to-all-start.1 = ((f32[8,800,128]{2,1,0:T(8,128)}), f32[8,800,128]{2,1,0:T(8,128)}, u32[]{:S(2)}, u32[]{:S(2)}) async-start(f32[8,800,128]{2,1,0:T(8,128)} %concatenate.78), calls=%async_computation.2 | async-start | bytes 6553600 | tf_op jit(solution)/shard_map/all_to_all | solution.py:621
  939.5 56.0 %copy-start.77 = (bf16[256,768,1]{1,0,2:T(8,128)(2,1)S(1)}, bf16[256,768,1]{1,0,2:T(8,128)(2,1)}, u32[]{:S(2)}) copy-start(bf16[256,768,1]{1,0,2:T(8,128)(2,1)} %reshape.1040) | copy-start | bytes 1179652
  1017.8 7.8 copy-start.161
  1017.8 7.8 copy-start.149
  1017.8 7.8 copy-start.150
  1017.8 7.8 copy-start.153
  1017.8 8.0 copy-start.124
  1025.7 10.6 copy-start.97
  1025.7 10.6 copy-start.133
  1025.7 10.6 copy-start.156
  1056.2 41.0 %all-to-all-start.2 = ((f32[3072,8,32]{0,2,1:T(8,128)}), f32[3072,8,32]{0,2,1:T(8,128)}, u32[]{:S(2)}, u32[]{:S(2)}) async-start(f32[3072,8,32]{0,2,1:T(8,128)} %all_to_all.39), calls=%async_computation.3 | async-start | bytes 6291456 | tf_op jit(solution)/shard_map/all_to_all | solution.py:625
  1105.6 61.1 %all-to-all-start.3 = ((f32[8,912,128]{2,1,0:T(8,128)}), f32[8,912,128]{2,1,0:T(8,128)}, u32[]{:S(2)}, u32[]{:S(2)}) async-start(f32[8,912,128]{2,1,0:T(8,128)} %constant_dynamic-update-slice_fusion.18), calls=%async_computation.4 | async-start | bytes 7471104 | tf_op jit(solution)/shard_map/all_to_all | solution.py:627
  1177.9 12.1 copy-start.164
  1177.9 21.4 %copy-start.148 = (f32[3,2,32]{2,1,0:T(2,128)S(1)}, f32[3,2,32]{2,1,0:T(2,128)}, u32[]{:S(2)}) copy-start(f32[3,2,32]{2,1,0:T(2,128)} %param.19) | copy-start | bytes 2308
  1177.9 22.0 %copy-start.32 = (f32[1,2,32,3,16,16]{5,4,3,2,1,0:T(8,128)S(1)}, f32[1,2,32,3,16,16]{5,4,3,2,1,0:T(8,128)}, u32[]{:S(2)}) copy-start(f32[1,2,32,3,16,16]{5,4,3,2,1,0:T(8,128)} %copy.178) | copy-start | bytes 589828
  1177.9 22.0 %copy-start.33 = (f32[1,2,32,3,16,16]{5,4,3,2,1,0:T(8,128)S(1)}, f32[1,2,32,3,16,16]{5,4,3,2,1,0:T(8,128)}, u32[]{:S(2)}) copy-start(f32[1,2,32,3,16,16]{5,4,3,2,1,0:T(8,128)} %copy.179) | copy-start | bytes 589828
  1213.5 7.8 copy-start.46
  (126 other events, 533.0 us)
Sparse Core Ops, SparseCore 0:
  14.5 31.4 all-gather.2
  120.0 122.0 all-gather.4
  748.5 315.7 reduce-scatter.1
